TPU v7x, 256 devices: a whole 4x4x8 slice. The times are simulated.
256 devices in a mesh: dp: 2 (over x_lo), space: 128 (over y, x_hi, z, core).
Axes of the slice: x: 4 (x_hi: 2, x_lo: 2; x = x_hi * 2 + x_lo), y: 4, z: 8, core: 2. Of those that a mesh axis runs over, the one named last changes fastest.
Arguments:
- activations: bfloat16 [4, 128, 64, 256], P('dp', 'space'), may hold values from -24 to 24
- out_grads: bfloat16 [4, 128, 64, 256], P('dp', 'space'), may hold values from -24 to 24
- old_input_factor: bfloat16 [2304, 2304], P(('dp', 'space')), may hold values from -3 to 3
- old_grad_factor: float32 [256, 256], P('space'), may hold values from -3 to 3
Outputs:
- input_factor: float32 [2304, 2304], P(('dp', 'space'))
- grad_factor: float32 [256, 256], P('space')
All inputs are finite; a program needn't handle non-finite values.
Results may differ from a plain program's by a relative error of at most 0.00055.
Values may be sent and summed in bfloat16 or wider, within the bound.
No kernel may reach another device: no remote copies, remote signals or barrier semaphores. Data moves between devices by JAX's collectives and lax.ppermute only.
A program may use at most 128 MiB of HBM per device.

v0:
```python
import jax
import jax.numpy as jnp
from jax import lax
from jax.sharding import Mesh
from jax.sharding import PartitionSpec as P

SPACE = ("space_0", "space_1", "space_2", "space_3")
DP_SPACE = ("dp", "space_0", "space_1", "space_2", "space_3")


def extended(block, sides, width):
    for axis, dim in sides:
        count = lax.axis_size(axis)
        forward = [(i, i + 1) for i in range(count - 1)]
        backward = [(target, source) for source, target in forward]
        low = lax.ppermute(
            lax.slice_in_dim(block, block.shape[dim] - width, None, axis=dim), axis, forward
        )
        high = lax.ppermute(lax.slice_in_dim(block, 0, width, axis=dim), axis, backward)
        block = jnp.concatenate([low, block, high], axis=dim)
    return block


def cut_along(array, dim, size):
    lengths = array.shape
    pieces = array.reshape(*lengths[:dim], size, lengths[dim] // size, *lengths[dim + 1 :])
    return jnp.moveaxis(pieces, dim, 0)


def sent_and_summed(array, axis, dim):
    pieces = cut_along(array, dim, lax.axis_size(axis))
    arrived = lax.all_to_all(pieces, axis, split_axis=0, concat_axis=0, tiled=True)
    return arrived.astype(jnp.float32).sum(axis=0)


def sum_by_axis(array, axes, dim):
    far, near = axes
    own = sent_and_summed(cut_along(array, dim, lax.axis_size(far)), near, dim + 1)
    return jnp.sum(
        lax.all_to_all(own.astype(jnp.bfloat16), far, 0, 0, tiled=True).astype(jnp.float32), axis=0
    )


def sent_and_summed_2(array, axis, dim):
    size = lax.axis_size(axis)
    pieces = lax.all_to_all(cut_along(array, dim, size), axis, 0, 0, tiled=True)
    return jnp.sum(pieces, axis=0)


def summed_rows(array, axes, dim):
    far, near = axes
    own = sent_and_summed_2(cut_along(array, dim, lax.axis_size(far)), near, dim + 1)
    return jnp.sum(lax.all_to_all(own, far, 0, 0, tiled=True), axis=0)


def copy_for_each(array, axis):
    copies = jnp.broadcast_to(array, (lax.axis_size(axis), *array.shape))
    return lax.all_to_all(copies, axis, split_axis=0, concat_axis=0, tiled=True)


def over_copies(array, axis):
    return copy_for_each(array, axis).sum(axis=0)


def transposed_product(left, right):
    return lax.dot_general(
        left, right, (((0,), (0,)), ((), ())), preferred_element_type=jnp.float32
    )


def per_device(activations, out_grads, old_input_factor, old_grad_factor):
    images, rows_here, columns_here, channels = activations.shape
    widened = extended(activations, ((SPACE, 1),), 1)
    padded = jnp.pad(widened, ((0, 0), (0, 0), (1, 1), (0, 0)))
    pieces = [
        padded[:, ky : ky + rows_here, kx : kx + columns_here, :]
        for ky in range(3)
        for kx in range(3)
    ]
    patches = jnp.concatenate(pieces, axis=3).reshape(
        images * rows_here * columns_here, 9 * channels
    )
    groups = lax.axis_size("dp")
    spaces = lax.axis_size(SPACE)
    positions = images * groups * rows_here * spaces * columns_here
    share = old_input_factor.shape[0]
    width_all = patches.shape[1]
    column_blocks = 4
    block_width = width_all // column_blocks
    results = []
    block = share * groups
    for which in range(column_blocks):
        right = patches[:, which * block_width : (which + 1) * block_width]

        def mapped_block(start, count, right=right):
            offsets = jnp.arange(count, dtype=jnp.int32)
            holder_space = offsets // block
            within_block = offsets % block
            holder_group = within_block // share
            within = within_block % share
            columns = holder_group * (spaces * share) + holder_space * share + within
            left = jnp.take(patches, columns, axis=1)
            return transposed_product(left, right)

        results.append(
            sum_by_axis(
                mapped_block(jnp.int32(0), block * lax.axis_size(SPACE)).astype(jnp.bfloat16),
                (("space_0", "space_1", "space_2"), "space_3"),
                0,
            )
        )
    part_sum = jnp.concatenate(results, axis=1)
    input_sum = sent_and_summed(part_sum.astype(jnp.bfloat16), "dp", 0)
    flat_grads = out_grads.reshape(images * rows_here * columns_here, channels)
    grad_term = transposed_product(flat_grads, flat_grads)
    grad_owned = summed_rows(grad_term, (("space_0", "space_1", "space_2"), "space_3"), 0)
    grad_sum = over_copies(grad_owned, "dp")
    input_factor = 0.5 * old_input_factor.astype(jnp.float32) + 0.5 / positions * input_sum
    grad_factor = 0.5 * old_grad_factor + 0.5 / positions * grad_sum
    return (input_factor, grad_factor)


def solution(mesh):
    finer = Mesh(
        mesh.devices.reshape(mesh.shape["dp"], 4, 2, 8, 2),
        ("dp", "space_0", "space_1", "space_2", "space_3"),
    )
    return jax.shard_map(
        per_device,
        mesh=finer,
        in_specs=(
            P("dp", SPACE, None, None),
            P("dp", SPACE, None, None),
            P(DP_SPACE, None),
            P(SPACE, None),
        ),
        out_specs=(P(DP_SPACE, None), P(SPACE, None)),
        check_vma=False,
    )
```

profile of v0, /device:TPU:32, one launch (start us, length us, event | category | flops | bytes accessed | tf_op | source)
XLA Modules:
  0.0 383.0 jit_solution(1361914128727010003)
XLA Ops:
  13.1 15.4 %all-to-all-start.10 = ((f32[64,2,256]{2,1,0:T(2,128)}), f32[64,2,256]{2,1,0:T(2,128)S(1)}, u32[]{:S(2)}, u32[]{:S(2)}) async-start(f32[64,2,256]{2,1,0:T(2,128)} %copy.100), calls=%async_computation.10 | async-start | bytes 262144 | tf_op jit(solution)/shard_map/all_to_all | solution.py:53
  30.0 4.7 %gather_fusion = bf16[2304,128]{1,0:T(8,128)(2,1)S(1)} fusion(bf16[128,2304]{0,1:T(8,128)(2,1)S(1)} %copy.85, s32[3072]{0:T(1024)S(1)} %pad_clamp_fusion), kind=kCustom, calls=%fused_computation.clone | custom fusion | bytes 1188864 | tf_op jit(solution)/shard_map/jit(_take)/gather | solution.py:102
  43.4 4.5 %copy.89 = bf16[2304,576]{1,0:T(8,128)(2,1)} copy(bf16[2304,576]{0,1:T(8,128)(2,1)} %convolution_convert_fusion.2) | data formatting | bytes 5308416 | tf_op jit(solution)/shard_map/convert_element_type | solution.py:107
  47.9 6.4 %reshape_reshape.14 = bf16[64,2,18,576]{3,2,1,0:T(8,128)(2,1)} reshape(bf16[2304,576]{1,0:T(8,128)(2,1)} %copy.89) | data formatting | bytes 5308416 | tf_op jit(solution)/shard_map/reshape;reshape | solution.py:26
  54.4 4.4 %copy.90 = bf16[2,64,18,576]{3,1,2,0:T(8,128)(2,1)} copy(bf16[2,64,18,576]{3,2,0,1:T(8,128)(2,1)} %bitcast.30) | data formatting | bytes 5308416 | tf_op jit(solution)/shard_map/transpose | solution.py:27
  58.7 4.5 %copy.92 = bf16[2304,576]{1,0:T(8,128)(2,1)} copy(bf16[2304,576]{0,1:T(8,128)(2,1)} %convolution_convert_fusion.1) | data formatting | bytes 5308416 | tf_op jit(solution)/shard_map/convert_element_type | solution.py:107
  63.2 6.4 %reshape_reshape.15 = bf16[64,2,18,576]{3,2,1,0:T(8,128)(2,1)} reshape(bf16[2304,576]{1,0:T(8,128)(2,1)} %copy.92) | data formatting | bytes 5308416 | tf_op jit(solution)/shard_map/reshape;reshape | solution.py:26
  69.7 4.4 %copy.93 = bf16[2,64,18,576]{3,1,2,0:T(8,128)(2,1)} copy(bf16[2,64,18,576]{3,2,0,1:T(8,128)(2,1)} %bitcast.31) | data formatting | bytes 5308416 | tf_op jit(solution)/shard_map/transpose | solution.py:27
  74.1 4.6 %copy.95 = bf16[2304,576]{1,0:T(8,128)(2,1)} copy(bf16[2304,576]{0,1:T(8,128)(2,1)} %convolution_convert_fusion) | data formatting | bytes 5308416 | tf_op jit(solution)/shard_map/convert_element_type | solution.py:107
  78.7 6.4 %reshape_reshape.16 = bf16[64,2,18,576]{3,2,1,0:T(8,128)(2,1)} reshape(bf16[2304,576]{1,0:T(8,128)(2,1)} %copy.95) | data formatting | bytes 5308416 | tf_op jit(solution)/shard_map/reshape;reshape | solution.py:26
  85.1 4.4 %copy.96 = bf16[2,64,18,576]{3,1,2,0:T(8,128)(2,1)} copy(bf16[2,64,18,576]{3,2,0,1:T(8,128)(2,1)} %bitcast.32) | data formatting | bytes 5308416 | tf_op jit(solution)/shard_map/transpose | solution.py:27
  99.4 4.4 %copy.87 = bf16[2,64,18,576]{3,1,2,0:T(8,128)(2,1)} copy(bf16[2,64,18,576]{3,2,0,1:T(8,128)(2,1)} %bitcast.33) | data formatting | bytes 5308416 | tf_op jit(solution)/shard_map/transpose | solution.py:27
  103.7 5.5 %all-to-all-start.2 = ((bf16[2,64,18,576]{3,1,2,0:T(8,128)(2,1)}), bf16[2,64,18,576]{3,1,2,0:T(8,128)(2,1)}, u32[]{:S(2)}, u32[]{:S(2)}) async-start(bf16[2,64,18,576]{3,1,2,0:T(8,128)(2,1)} %copy.90), calls=%async_computation.2 | async-start | bytes 5898240 | tf_op jit(solution)/shard_map/all_to_all | solution.py:32
  112.8 7.4 %all_to_all.61 = bf16[2,64,18,576]{3,1,2,0:T(8,128)(2,1)} all-to-all(bf16[2,64,18,576]{3,1,2,0:T(8,128)(2,1)S(1)} %copy-done), channel_id=1, replica_groups=mesh['dp'=2,'space_0'=4,'space_1'=2,'space_2'=8,'space_3'=2] {'space_3'}, dimensions={0} | all-to-all | bytes 5308416 | tf_op jit(solution)/shard_map/all_to_all | solution.py:32
  120.2 7.3 %all_to_all.62 = bf16[2,64,18,576]{3,1,2,0:T(8,128)(2,1)} all-to-all(bf16[2,64,18,576]{3,1,2,0:T(8,128)(2,1)S(1)} %copy-done.1), channel_id=1, replica_groups=mesh['dp'=2,'space_0'=4,'space_1'=2,'space_2'=8,'space_3'=2] {'space_3'}, dimensions={0} | all-to-all | bytes 5308416 | tf_op jit(solution)/shard_map/all_to_all | solution.py:32
  127.5 6.1 %all_to_all.63 = bf16[2,64,18,576]{3,1,2,0:T(8,128)(2,1)S(1)} all-to-all(bf16[2,64,18,576]{3,1,2,0:T(8,128)(2,1)S(1)} %copy-done.2), channel_id=1, replica_groups=mesh['dp'=2,'space_0'=4,'space_1'=2,'space_2'=8,'space_3'=2] {'space_3'}, dimensions={0} | all-to-all | bytes 5308416 | tf_op jit(solution)/shard_map/all_to_all | solution.py:32
  145.0 12.9 %all-to-all-start.3 = ((bf16[64,18,576]{2,1,0:T(8,128)(2,1)}), bf16[64,18,576]{2,1,0:T(8,128)(2,1)}, u32[]{:S(2)}, u32[]{:S(2)}) async-start(bf16[64,18,576]{2,1,0:T(8,128)(2,1)} %copy.91), calls=%async_computation.3 | async-start | bytes 3932160 | tf_op jit(solution)/shard_map/all_to_all | solution.py:40
  165.5 41.9 %all-to-all-done.3 = bf16[64,18,576]{2,1,0:T(8,128)(2,1)} async-done(((bf16[64,18,576]{2,1,0:T(8,128)(2,1)}), bf16[64,18,576]{2,1,0:T(8,128)(2,1)}, u32[]{:S(2)}, u32[]{:S(2)}) %all-to-all-start.3) | async-done | bytes 1327136 | tf_op jit(solution)/shard_map/all_to_all | solution.py:40
  207.4 7.1 %all-to-all-start.5 = ((bf16[64,18,576]{2,1,0:T(8,128)(2,1)}), bf16[64,18,576]{2,1,0:T(8,128)(2,1)}, u32[]{:S(2)}, u32[]{:S(2)}) async-start(bf16[64,18,576]{2,1,0:T(8,128)(2,1)} %copy.94), calls=%async_computation.5 | async-start | bytes 3932160 | tf_op jit(solution)/shard_map/all_to_all | solution.py:40
  222.0 41.3 %all-to-all-done.5 = bf16[64,18,576]{2,1,0:T(8,128)(2,1)} async-done(((bf16[64,18,576]{2,1,0:T(8,128)(2,1)}), bf16[64,18,576]{2,1,0:T(8,128)(2,1)}, u32[]{:S(2)}, u32[]{:S(2)}) %all-to-all-start.5) | async-done | bytes 1327136 | tf_op jit(solution)/shard_map/all_to_all | solution.py:40
  263.3 6.7 %all-to-all-start.7 = ((bf16[64,18,576]{2,1,0:T(8,128)(2,1)}), bf16[64,18,576]{2,1,0:T(8,128)(2,1)}, u32[]{:S(2)}, u32[]{:S(2)}) async-start(bf16[64,18,576]{2,1,0:T(8,128)(2,1)} %copy.97), calls=%async_computation.7 | async-start | bytes 3932160 | tf_op jit(solution)/shard_map/all_to_all | solution.py:40
  275.8 42.6 %all-to-all-done.7 = bf16[64,18,576]{2,1,0:T(8,128)(2,1)} async-done(((bf16[64,18,576]{2,1,0:T(8,128)(2,1)}), bf16[64,18,576]{2,1,0:T(8,128)(2,1)}, u32[]{:S(2)}, u32[]{:S(2)}) %all-to-all-start.7) | async-done | bytes 1327136 | tf_op jit(solution)/shard_map/all_to_all | solution.py:40
  318.4 6.5 %all-to-all-start.1 = ((bf16[64,18,576]{2,1,0:T(8,128)(2,1)}), bf16[64,18,576]{2,1,0:T(8,128)(2,1)S(1)}, u32[]{:S(2)}, u32[]{:S(2)}) async-start(bf16[64,18,576]{2,1,0:T(8,128)(2,1)} %copy.88), calls=%async_computation.1 | async-start | bytes 3932160 | tf_op jit(solution)/shard_map/all_to_all | solution.py:40
  330.8 42.3 %all-to-all-done.1 = bf16[64,18,576]{2,1,0:T(8,128)(2,1)S(1)} async-done(((bf16[64,18,576]{2,1,0:T(8,128)(2,1)}), bf16[64,18,576]{2,1,0:T(8,128)(2,1)S(1)}, u32[]{:S(2)}, u32[]{:S(2)}) %all-to-all-start.1) | async-done | bytes 1327136 | tf_op jit(solution)/shard_map/all_to_all | solution.py:40
  (70 shorter events, 83.8 us)
Async XLA Ops:
  0.6 29.0 %copy-start.3 = (bf16[2,1,64,256]{3,2,1,0:T(8,128)(2,1)S(1)}, bf16[2,1,64,256]{3,2,1,0:T(8,128)(2,1)}, u32[]{:S(2)}) copy-start(bf16[2,1,64,256]{3,2,1,0:T(8,128)(2,1)} %param.6) | copy-start | bytes 196612
  0.6 27.9 %collective-permute-start = (bf16[2,1,64,256]{3,2,0,1:T(8,128)(2,1)}, bf16[2,1,64,256]{3,2,0,1:T(8,128)(2,1)S(1)}, u32[]{:S(2)}, u32[]{:S(2)}) collective-permute-start(bf16[2,1,64,256]{3,2,0,1:T(8,128)(2,1)} %bitcast.39), channel_id=1, source_target_pairs={{0,1},{1,2},{2,3},{3,4},{4,5},{5,6},{6,7},{7,8},{8,9},{9,10},{10,1... | collective-permute-start | bytes 196616 | tf_op jit(solution)/shard_map/ppermute | solution.py:16
  2.7 25.9 %collective-permute-start.1 = (bf16[2,1,64,256]{3,2,0,1:T(8,128)(2,1)}, bf16[2,1,64,256]{3,2,0,1:T(8,128)(2,1)S(1)}, u32[]{:S(2)}, u32[]{:S(2)}) collective-permute-start(bf16[2,1,64,256]{3,2,0,1:T(8,128)(2,1)} %bitcast.40), channel_id=1, source_target_pairs={{1,0},{2,1},{3,2},{4,3},{5,4},{6,5},{7,6},{8,7},{9,8},{10,9},{11,1... | collective-permute-start | bytes 196616 | tf_op jit(solution)/shard_map/ppermute | solution.py:19
  13.1 90.7 %all-to-all-start.10 = ((f32[64,2,256]{2,1,0:T(2,128)}), f32[64,2,256]{2,1,0:T(2,128)S(1)}, u32[]{:S(2)}, u32[]{:S(2)}) async-start(f32[64,2,256]{2,1,0:T(2,128)} %copy.100), calls=%async_computation.10 | async-start | bytes 262144 | tf_op jit(solution)/shard_map/all_to_all | solution.py:53
  103.7 9.1 %copy-start = (bf16[2,64,18,576]{3,1,2,0:T(8,128)(2,1)S(1)}, bf16[2,64,18,576]{3,1,2,0:T(8,128)(2,1)}, u32[]{:S(2)}) copy-start(bf16[2,64,18,576]{3,1,2,0:T(8,128)(2,1)} %copy.93) | copy-start | bytes 7962628
  103.7 9.1 %all-to-all-start.2 = ((bf16[2,64,18,576]{3,1,2,0:T(8,128)(2,1)}), bf16[2,64,18,576]{3,1,2,0:T(8,128)(2,1)}, u32[]{:S(2)}, u32[]{:S(2)}) async-start(bf16[2,64,18,576]{3,1,2,0:T(8,128)(2,1)} %copy.90), calls=%async_computation.2 | async-start | bytes 5898240 | tf_op jit(solution)/shard_map/all_to_all | solution.py:32
  112.8 7.4 %copy-start.1 = (bf16[2,64,18,576]{3,1,2,0:T(8,128)(2,1)S(1)}, bf16[2,64,18,576]{3,1,2,0:T(8,128)(2,1)}, u32[]{:S(2)}) copy-start(bf16[2,64,18,576]{3,1,2,0:T(8,128)(2,1)} %copy.96) | copy-start | bytes 7962628
  120.2 7.3 %copy-start.2 = (bf16[2,64,18,576]{3,1,2,0:T(8,128)(2,1)S(1)}, bf16[2,64,18,576]{3,1,2,0:T(8,128)(2,1)}, u32[]{:S(2)}) copy-start(bf16[2,64,18,576]{3,1,2,0:T(8,128)(2,1)} %copy.87) | copy-start | bytes 7962628
  134.2 10.8 %all-to-all-start.11 = ((f32[2,2,256]{2,1,0:T(2,128)}), f32[2,2,256]{2,1,0:T(2,128)S(1)}, u32[]{:S(2)}, u32[]{:S(2)}) async-start(f32[2,2,256]{2,1,0:T(2,128)} %broadcast_in_dim.12), calls=%async_computation.11 | async-start | bytes 8192 | tf_op jit(solution)/shard_map/all_to_all | solution.py:58
  145.0 62.4 %all-to-all-start.3 = ((bf16[64,18,576]{2,1,0:T(8,128)(2,1)}), bf16[64,18,576]{2,1,0:T(8,128)(2,1)}, u32[]{:S(2)}, u32[]{:S(2)}) async-start(bf16[64,18,576]{2,1,0:T(8,128)(2,1)} %copy.91), calls=%async_computation.3 | async-start | bytes 3932160 | tf_op jit(solution)/shard_map/all_to_all | solution.py:40
  207.4 56.0 %all-to-all-start.5 = ((bf16[64,18,576]{2,1,0:T(8,128)(2,1)}), bf16[64,18,576]{2,1,0:T(8,128)(2,1)}, u32[]{:S(2)}, u32[]{:S(2)}) async-start(bf16[64,18,576]{2,1,0:T(8,128)(2,1)} %copy.94), calls=%async_computation.5 | async-start | bytes 3932160 | tf_op jit(solution)/shard_map/all_to_all | solution.py:40
  263.3 55.1 %all-to-all-start.7 = ((bf16[64,18,576]{2,1,0:T(8,128)(2,1)}), bf16[64,18,576]{2,1,0:T(8,128)(2,1)}, u32[]{:S(2)}, u32[]{:S(2)}) async-start(bf16[64,18,576]{2,1,0:T(8,128)(2,1)} %copy.97), calls=%async_computation.7 | async-start | bytes 3932160 | tf_op jit(solution)/shard_map/all_to_all | solution.py:40
  318.4 54.7 %all-to-all-start.1 = ((bf16[64,18,576]{2,1,0:T(8,128)(2,1)}), bf16[64,18,576]{2,1,0:T(8,128)(2,1)S(1)}, u32[]{:S(2)}, u32[]{:S(2)}) async-start(bf16[64,18,576]{2,1,0:T(8,128)(2,1)} %copy.88), calls=%async_computation.1 | async-start | bytes 3932160 | tf_op jit(solution)/shard_map/all_to_all | solution.py:40
  326.9 50.8 %copy-start.5 = (f32[2,256]{1,0:T(2,128)S(1)}, f32[2,256]{1,0:T(2,128)}, u32[]{:S(2)}) copy-start(f32[2,256]{1,0:T(2,128)} %param.9) | copy-start | bytes 6148
  328.8 53.4 %copy-start.4 = (bf16[9,2304]{1,0:T(8,128)(2,1)S(1)}, bf16[9,2304]{1,0:T(8,128)(2,1)}, u32[]{:S(2)}) copy-start(bf16[9,2304]{1,0:T(8,128)(2,1)} %param.8) | copy-start | bytes 124420
  374.3 8.0 %all-to-all-start.8 = ((bf16[2,9,2304]{2,1,0:T(8,128)(2,1)}), bf16[2,9,2304]{2,1,0:T(8,128)(2,1)S(1)}, u32[]{:S(2)}, u32[]{:S(2)}) async-start(bf16[2,9,2304]{2,1,0:T(8,128)(2,1)} %concatenate.25), calls=%async_computation.8 | async-start | bytes 294912 | tf_op jit(solution)/shard_map/all_to_all | solution.py:32
where the time goes:
time: 385 us; the launch traced here: 383 us
  waiting for transfers between devices  176 us (46%)
  local copies, waits for them, and re-layouts  80 us (21%)
  starting transfers between devices  66.5 us (17%)
  blocking collectives  24.7 us (6%)
  other arithmetic  22.5 us (6%)
  matrix products  12.7 us (3%)
    all_to_all x4, waiting for transfers between devices, sum_by_axis(): lax.all_to_all(own.astype(jnp.bfloat16), far, 0, 0, tiled=True)  168 us
    all_to_all x4, starting transfers between devices, sum_by_axis(): lax.all_to_all(own.astype(jnp.bfloat16), far, 0, 0, tiled=True)  33.2 us
    another operation x4, local copies, waits for them, and re-layouts, cut_along(): array.reshape(*lengths[:dim], size, lengths[dim] // size, *lengths[dim +...  22.1 us
    all_to_all x3, blocking collectives, sent_and_summed(): lax.all_to_all(pieces, axis, split_axis=0, concat_axis=0, tiled=True)  20.8 us
    transpose x4, local copies, waits for them, and re-layouts, cut_along(): return jnp.moveaxis(pieces, dim, 0)  17.6 us
    convert_element_type x4, local copies, waits for them, and re-layouts, per_device(): mapped_block(jnp.int32(0), block * lax.axis_size(SPACE))  17.6 us
    all_to_all x1, starting transfers between devices, summed_rows(): return jnp.sum(lax.all_to_all(own, far, 0, 0, tiled=True), axis=0)  15.4 us
    reduce_sum x4, local copies, waits for them, and re-layouts, sent_and_summed(): return arrived.astype(jnp.float32).sum(axis=0)  14.3 us
  transfers between devices with their start and end apart: 10, of which 6 were waited for; matrix products, arithmetic and copies ran while one was open for 29% of the time, Pallas kernels for 0%

commit v1 on v0

v1 whole, which is shorter than its diff:
```python
import jax
import jax.numpy as jnp
from jax import lax
from jax.experimental import pallas as pl
from jax.experimental.pallas import tpu as pltpu
from jax.sharding import Mesh
from jax.sharding import PartitionSpec as P

SPACE = ("y", "xh", "z", "c")
DP_SPACE = ("dp", "y", "xh", "z", "c")
Q = ("dp", "y", "xh")
ROW = 128
CH = 256
KK = 9 * CH
F32 = jnp.float32
BF16 = jnp.bfloat16
EXT = 512
WIDE = KK + EXT


def fan_kernel(a_ref, g_ref, out_ref, part):
    a = a_ref[...]
    g = g_ref[...]
    part[...] = lax.dot_general(g, g, (((0,), (0,)), ((), ())), preferred_element_type=F32)
    for z in range(8):
        out_ref[z, :ROW, :] = a
        rows = [part[32 * q + 4 * z : 32 * q + 4 * z + 4, :] for q in range(8)]
        out_ref[z, ROW:, :] = jnp.concatenate(rows, axis=0).astype(BF16)


def main_kernel(idx, got, oth, lo, hi, out, v, sel, lt, ext, gs):
    g = idx[0]
    c = idx[1]
    pos = lax.broadcasted_iota(jnp.int32, (ROW, CH), 0) % 64

    def put(x, row):
        at = pl.ds(pl.multiple_of(row * ROW, ROW), ROW)
        xf = x.astype(F32)
        v[1, at, :] = x
        v[0, at, :] = jnp.where(pos == 0, 0.0, pltpu.roll(xf, 1, 0)).astype(BF16)
        v[2, at, :] = jnp.where(pos == 63, 0.0, pltpu.roll(xf, ROW - 1, 0)).astype(BF16)

    put(lo[...], 0)
    put(hi[...], 17)

    def rows_of(z, carry):
        put(got[z, :ROW, :], 1 + 2 * z + c)
        put(oth[z, :ROW, :], 2 + 2 * z - c)
        return carry

    lax.fori_loop(0, 8, rows_of, 0)

    m = lax.broadcasted_iota(jnp.int32, (144, CH), 0)
    lane = lax.broadcasted_iota(jnp.int32, (144, CH), 1)
    owner = jnp.where(m < 128, m // 8, m - 128)
    within = jnp.where(m < 128, m % 8, 8)
    channel = owner * 144 + within + g * 9 - lane
    for t in range(9):
        sel[t] = jnp.where(channel == t * CH, 1.0, 0.0).astype(BF16)
    for n in range(8):
        acc = None
        for t in range(9):
            ky, kx = divmod(t, 3)
            part = lax.dot_general(
                sel[t],
                v[kx, ky * ROW + n * 256 : ky * ROW + n * 256 + 256, :],
                (((1,), (1,)), ((), ())),
                preferred_element_type=F32,
            )
            acc = part if acc is None else acc + part
        lt[:, n * 256 : n * 256 + 256] = acc.astype(BF16)

    ext[...] = jnp.zeros_like(ext)
    for t in range(9):
        ky, kx = divmod(t, 3)
        res = jnp.dot(lt[...], v[kx, ky * ROW : ky * ROW + 16 * ROW, :], preferred_element_type=F32)
        out[:, :, t * CH : t * CH + CH] = res[:128].reshape(16, 8, CH).astype(BF16)
        for q in range(16):
            ext[q, t // 2 : t // 2 + 1, (t % 2) * CH : (t % 2) * CH + CH] = res[128 + q : 129 + q]

    total = jnp.zeros((32, CH), F32)
    for z in range(8):
        total += got[z, ROW:, :].astype(F32) + oth[z, ROW:, :].astype(F32)
    gs[...] = total
    for q in range(16):
        for r in range(2):
            row = gs[pl.ds((q % 8) * 4 + r + 2 * c, 1), :]
            high = row.astype(BF16).astype(F32)
            ext[q, 5:6, r * CH : r * CH + CH] = high
            ext[q, 6:7, r * CH : r * CH + CH] = row - high
    out[:, :, KK:] = ext[...].astype(BF16)


def end_kernel(coef, got, old_in, old_g, out_in, out_g):
    total = got[0].astype(F32)
    for q in range(1, 16):
        total += got[q].astype(F32)
    out_in[0:8, :] = 0.5 * old_in[0:8, :].astype(F32) + coef * total[:, :KK]
    last = 0.5 * old_in[8:9, :].astype(F32)
    for i in range(9):
        at = KK + (i % 2) * CH
        out_in[8:9, i * CH : i * CH + CH] = (
            last[:, i * CH : i * CH + CH] + coef * total[i // 2 : i // 2 + 1, at : at + CH]
        )
    for r in range(2):
        at = KK + r * CH
        out_g[r : r + 1, :] = 0.5 * old_g[r : r + 1, :] + coef * (
            total[5:6, at : at + CH] + total[6:7, at : at + CH]
        )


def per_device(activations, out_grads, old_input_factor, old_grad_factor):
    images, rows_here, columns_here, channels = activations.shape
    positions = images * lax.axis_size("dp") * rows_here * lax.axis_size(SPACE) * columns_here
    a = activations.reshape(ROW, CH)
    g = out_grads.reshape(ROW, CH)
    c = lax.axis_index("c")
    index = jnp.stack([lax.axis_index("z") * 2 + c, c]).astype(jnp.int32)
    vmem = pl.BlockSpec(memory_space=pltpu.VMEM)
    smem = pl.BlockSpec(memory_space=pltpu.SMEM)
    sent = pl.pallas_call(
        fan_kernel,
        out_shape=jax.ShapeDtypeStruct((8, ROW + 32, CH), BF16),
        in_specs=[vmem, vmem],
        out_specs=vmem,
        scratch_shapes=[pltpu.VMEM((CH, CH), F32)],
    )(a, g)
    got = lax.all_to_all(sent, "z", 0, 0, tiled=True)
    oth = lax.ppermute(got, "c", [(0, 1), (1, 0)])
    first = jnp.where(c == 0, got[0, :ROW], oth[0, :ROW])
    last = jnp.where(c == 1, got[7, :ROW], oth[7, :ROW])
    lo = lax.ppermute(last, ("y", "xh"), [(i, i + 1) for i in range(7)])
    hi = lax.ppermute(first, ("y", "xh"), [(i + 1, i) for i in range(7)])
    parts = pl.pallas_call(
        main_kernel,
        out_shape=jax.ShapeDtypeStruct((16, 8, WIDE), BF16),
        in_specs=[smem, vmem, vmem, vmem, vmem],
        out_specs=vmem,
        scratch_shapes=[
            pltpu.VMEM((3, 18 * ROW, CH), BF16),
            pltpu.VMEM((9, 144, CH), BF16),
            pltpu.VMEM((144, 16 * ROW), BF16),
            pltpu.VMEM((16, 8, EXT), F32),
            pltpu.VMEM((32, CH), F32),
        ],
        cost_estimate=pl.CostEstimate(flops=3_000_000_000, bytes_accessed=3_000_000, transcendentals=0),
    )(index, got, oth, lo, hi)
    arrived = lax.all_to_all(parts, Q, 0, 0, tiled=True)
    return tuple(
        pl.pallas_call(
            lambda *refs: end_kernel(0.5 / positions, *refs),
            out_shape=(
                jax.ShapeDtypeStruct((9, KK), F32),
                jax.ShapeDtypeStruct((2, CH), F32),
            ),
            in_specs=[vmem, vmem, vmem],
            out_specs=(vmem, vmem),
        )(arrived, old_input_factor, old_grad_factor)
    )


def solution(mesh):
    finer = Mesh(
        mesh.devices.reshape(mesh.shape["dp"], 4, 2, 8, 2),
        ("dp", "y", "xh", "z", "c"),
    )
    return jax.shard_map(
        per_device,
        mesh=finer,
        in_specs=(
            P("dp", SPACE, None, None),
            P("dp", SPACE, None, None),
            P(DP_SPACE, None),
            P(SPACE, None),
        ),
        out_specs=(P(DP_SPACE, None), P(SPACE, None)),
        check_vma=False,
    )
```

time: 385 us -> 73.7 us (0.19)
  waiting for transfers between devices: 176 us -> 3.32 us
  local copies, waits for them, and re-layouts: 80 us -> 0.64 us
  starting transfers between devices: 66.5 us -> 7.35 us
  blocking collectives: 24.7 us -> 49 us
  other arithmetic: 22.5 us -> 0.67 us
  matrix products: 12.7 us -> 0 us
  Pallas kernels: 0 us -> 11.4 us
    all_to_all x8 -> x0, waiting for transfers between devices: 176 us -> none  [the longest x4 168 us: sum_by_axis(): lax.all_to_all(own.astype(jnp.bfloat16), far, 0, 0, tiled=True)]
    all_to_all x8 -> x0, starting transfers between devices: 60.8 us -> none  [the longest x4 33.2 us: sum_by_axis(): lax.all_to_all(own.astype(jnp.bfloat16), far, 0, 0, tiled=True)]
    all_to_all x4 -> x2, blocking collectives: 24.7 us -> 49 us  [the longest x1 27.4 us: per_device(): got = lax.all_to_all(sent, 'z', 0, 0, tiled=True)]
    another operation x4 -> x0, local copies, waits for them, and re-layouts: 22.1 us -> none  [cut_along(): array.reshape(*lengths[:dim], size, lengths[dim] // size, *lengths[dim +...]
    reduce_sum x12 -> x0, other arithmetic: 20.3 us -> none  [the longest x5 14.1 us: sent_and_summed(): return arrived.astype(jnp.float32).sum(axis=0)]
    transpose x4 -> x0, local copies, waits for them, and re-layouts: 17.6 us -> none  [cut_along(): return jnp.moveaxis(pieces, dim, 0)]
    convert_element_type x4 -> x0, local copies, waits for them, and re-layouts: 17.6 us -> none  [per_device(): mapped_block(jnp.int32(0), block * lax.axis_size(SPACE))]
    reduce_sum x5 -> x0, local copies, waits for them, and re-layouts: 15.1 us -> none  [the longest x4 14.3 us: sent_and_summed(): return arrived.astype(jnp.float32).sum(axis=0)]
  transfers between devices with their start and end apart: 10 -> 3, of which waited for: 6 -> 2; matrix products, arithmetic and copies ran while one was open for 29% -> 1% of each run, Pallas kernels for 0% -> 0%
where the time goes in v1:
time: 73.7 us; the launch traced here: 73 us
  blocking collectives  49 us (66%)
  Pallas kernels  11.4 us (15%)
  starting transfers between devices  7.35 us (10%)
  waiting for transfers between devices  3.32 us (5%)
    all_to_all x1, blocking collectives, per_device(): got = lax.all_to_all(sent, 'z', 0, 0, tiled=True)  27.4 us
    all_to_all x1, blocking collectives, per_device(): arrived = lax.all_to_all(parts, Q, 0, 0, tiled=True)  21.5 us
    pallas_call x1, Pallas kernels, per_device(): pl.pallas_call(main_kernel, out_shape=jax.ShapeDtypeStruct((16, 8, WIDE),...  7.53 us
    ppermute x1, starting transfers between devices, per_device(): lo = lax.ppermute(last, ('y', 'xh'), [(i, i + 1) for i in range(7)])  6.05 us
    ppermute x1, waiting for transfers between devices, per_device(): oth = lax.ppermute(got, 'c', [(0, 1), (1, 0)])  2.09 us
    pallas_call x1, Pallas kernels, per_device(): pl.pallas_call(fan_kernel, out_shape=jax.ShapeDtypeStruct((8, ROW + 32, C...  1.94 us
    pallas_call x1, Pallas kernels, per_device(): pl.pallas_call(lambda *refs: end_kernel(0.5 / positions, *refs), out_shap...  1.94 us
  transfers between devices with their start and end apart: 3, of which 2 were waited for; matrix products, arithmetic and copies ran while one was open for 1% of the time, Pallas kernels for 0%

profile of v1, /device:TPU:32, one launch (start us, length us, event | category | flops | bytes accessed | tf_op | source)
XLA Modules:
  0.0 73.0 jit_solution(6257136623552281181)
XLA Ops:
  0.6 1.9 %shard_map.59 = bf16[8,160,256]{2,1,0:T(8,128)(2,1)} custom-call(bf16[128,256]{1,0:T(8,128)(2,1)} %bitcast.8, bf16[128,256]{1,0:T(8,128)(2,1)} %bitcast.9), custom_call_target="tpu_custom_call" | custom-call | tf_op jit(solution)/shard_map/pallas_call | solution.py:121
  2.6 27.4 %all_to_all.10.got = bf16[8,160,256]{2,1,0:T(8,128)(2,1)S(1)} all-to-all(bf16[8,160,256]{2,1,0:T(8,128)(2,1)} %shard_map.59), channel_id=1, replica_groups=mesh['dp'=2,'y'=4,'xh'=2,'z'=8,'c'=2] {'z'}, dimensions={0} | all-to-all | bytes 1310720 | tf_op jit(solution)/shard_map/all_to_all | solution.py:128
  30.0 0.0 copy-start
  30.0 0.0 collective-permute-start
  30.0 2.1 %collective-permute-done.oth = bf16[8,160,256]{2,1,0:T(8,128)(2,1)S(1)} collective-permute-done((bf16[8,160,256]{2,1,0:T(8,128)(2,1)S(1)}, bf16[8,160,256]{2,1,0:T(8,128)(2,1)S(1)}, u32[]{:S(2)}, u32[]{:S(2)}) %collective-permute-start) | collective-permute-done | bytes 655392 | tf_op jit(solution)/shard_map/ppermute | solution.py:129
  32.1 0.0 copy-start.1
  32.1 1.3 %collective-permute-start.2 = (bf16[128,256]{1,0:T(8,128)(2,1)S(1)}, bf16[128,256]{1,0:T(8,128)(2,1)S(1)}, u32[]{:S(2)}, u32[]{:S(2)}) collective-permute-start(bf16[128,256]{1,0:T(8,128)(2,1)S(1)} %get-tuple-element.2), channel_id=1, source_target_pairs={{16,0},{32,16},{48,32},{64,48},{80,64},{96,80},{112,96},{17,1},{33... | collective-permute-start | bytes 196616 | tf_op jit(solution)/shard_map/ppermute | solution.py:133
  33.4 6.1 %collective-permute-start.1 = (bf16[128,256]{1,0:T(8,128)(2,1)S(1)}, bf16[128,256]{1,0:T(8,128)(2,1)S(1)}, u32[]{:S(2)}, u32[]{:S(2)}) collective-permute-start(bf16[128,256]{1,0:T(8,128)(2,1)S(1)} %get-tuple-element.3), channel_id=1, source_target_pairs={{0,16},{16,32},{32,48},{48,64},{64,80},{80,96},{96,112},{1,17},{17... | collective-permute-start | bytes 196616 | tf_op jit(solution)/shard_map/ppermute | solution.py:132
  39.5 0.7 pad_add_fusion.idx
  40.1 0.0 collective-permute-done.2.hi
  40.1 0.0 copy-start.2
  40.1 1.2 %collective-permute-done.1.lo = bf16[128,256]{1,0:T(8,128)(2,1)S(1)} collective-permute-done((bf16[128,256]{1,0:T(8,128)(2,1)S(1)}, bf16[128,256]{1,0:T(8,128)(2,1)S(1)}, u32[]{:S(2)}, u32[]{:S(2)}) %collective-permute-start.1) | collective-permute-done | bytes 65568 | tf_op jit(solution)/shard_map/ppermute | solution.py:132
  41.3 0.0 copy-done
  41.3 0.0 copy-done.1
  41.4 0.0 copy-done.2
  41.4 0.0 copy-start.3
  41.4 0.6 copy-done.3
  42.0 7.5 %shard_map.60 = bf16[16,8,2816]{2,1,0:T(8,128)(2,1)} custom-call(s32[2]{0:T(128)} %pad_add_fusion.idx, bf16[8,160,256]{2,1,0:T(8,128)(2,1)} %copy-done, bf16[8,160,256]{2,1,0:T(8,128)(2,1)} %copy-done.1, bf16[128,256]{1,0:T(8,128)(2,1)} %copy-done.3, bf16[128,256]{1,0:T(8,128)(2,1)} %copy-done.2), custom_call_target="tpu_custom_call" | custom-call | flops 3000000000 | bytes 3000000 | tf_op jit(solution)/shard_map/pallas_call | solution.py:134
  49.5 21.5 %all_to_all.11.refs_0_ = bf16[16,8,2816]{2,1,0:T(8,128)(2,1)} all-to-all(bf16[16,8,2816]{2,1,0:T(8,128)(2,1)} %shard_map.60), channel_id=1, replica_groups=mesh['dp'=2,'y'=4,'xh'=2,'z'=8,'c'=2] {'dp','y','xh'}, dimensions={0} | all-to-all | bytes 1441792 | tf_op jit(solution)/shard_map/all_to_all | solution.py:148
  71.1 1.9 %shard_map.61 = (f32[9,2304]{1,0:T(8,128)}, f32[2,256]{1,0:T(2,128)}) custom-call(bf16[16,8,2816]{2,1,0:T(8,128)(2,1)} %all_to_all.11.refs_0_, bf16[9,2304]{1,0:T(8,128)(2,1)} %refs_1_.1, f32[2,256]{1,0:T(2,128)} %refs_2_.1), custom_call_target="tpu_custom_call" | custom-call | tf_op jit(solution)/shard_map/pallas_call | solution.py:150
  (1 shorter events, 0.0 us)
Async XLA Ops:
  30.0 11.4 %copy-start = (bf16[8,160,256]{2,1,0:T(8,128)(2,1)}, bf16[8,160,256]{2,1,0:T(8,128)(2,1)S(1)}, u32[]{:S(2)}) copy-start(bf16[8,160,256]{2,1,0:T(8,128)(2,1)S(1)} %all_to_all.10.got) | copy-start | bytes 1966084
  30.0 2.1 %collective-permute-start = (bf16[8,160,256]{2,1,0:T(8,128)(2,1)S(1)}, bf16[8,160,256]{2,1,0:T(8,128)(2,1)S(1)}, u32[]{:S(2)}, u32[]{:S(2)}) collective-permute-start(bf16[8,160,256]{2,1,0:T(8,128)(2,1)S(1)} %all_to_all.10.got), channel_id=1, source_target_pairs={{0,1},{1,0},{2,3},{3,2},{4,5},{5,4},{6,7},{7,6},{8,9},{9,8},{10,11... | collective-permute-start | bytes 1966088 | tf_op jit(solution)/shard_map/ppermute | solution.py:129
  32.1 9.3 %copy-start.1 = (bf16[8,160,256]{2,1,0:T(8,128)(2,1)}, bf16[8,160,256]{2,1,0:T(8,128)(2,1)S(1)}, u32[]{:S(2)}) copy-start(bf16[8,160,256]{2,1,0:T(8,128)(2,1)S(1)} %collective-permute-done.oth) | copy-start | bytes 1966084
  32.1 8.0 %collective-permute-start.2 = (bf16[128,256]{1,0:T(8,128)(2,1)S(1)}, bf16[128,256]{1,0:T(8,128)(2,1)S(1)}, u32[]{:S(2)}, u32[]{:S(2)}) collective-permute-start(bf16[128,256]{1,0:T(8,128)(2,1)S(1)} %get-tuple-element.2), channel_id=1, source_target_pairs={{16,0},{32,16},{48,32},{64,48},{80,64},{96,80},{112,96},{17,1},{33... | collective-permute-start | bytes 196616 | tf_op jit(solution)/shard_map/ppermute | solution.py:133
  33.4 7.9 %collective-permute-start.1 = (bf16[128,256]{1,0:T(8,128)(2,1)S(1)}, bf16[128,256]{1,0:T(8,128)(2,1)S(1)}, u32[]{:S(2)}, u32[]{:S(2)}) collective-permute-start(bf16[128,256]{1,0:T(8,128)(2,1)S(1)} %get-tuple-element.3), channel_id=1, source_target_pairs={{0,16},{16,32},{32,48},{48,64},{64,80},{80,96},{96,112},{1,17},{17... | collective-permute-start | bytes 196616 | tf_op jit(solution)/shard_map/ppermute | solution.py:132
  40.1 1.2 %copy-start.2 = (bf16[128,256]{1,0:T(8,128)(2,1)}, bf16[128,256]{1,0:T(8,128)(2,1)S(1)}, u32[]{:S(2)}) copy-start(bf16[128,256]{1,0:T(8,128)(2,1)S(1)} %collective-permute-done.2.hi) | copy-start | bytes 196612
  41.4 0.6 copy-start.3

commit v2 on v1

v2 whole, which is shorter than its diff:
```python
import jax
import jax.numpy as jnp
from jax import lax
from jax.experimental import pallas as pl
from jax.experimental.pallas import tpu as pltpu
from jax.sharding import Mesh
from jax.sharding import PartitionSpec as P


SPACE = ("y", "xh", "z", "c")
DP_SPACE = ("dp", "y", "xh", "z", "c")
Q = ("dp", "y", "xh")
ROW = 128
CH = 256
KK = 9 * CH
F32 = jnp.float32
BF16 = jnp.bfloat16
EXT = 512
WIDE = KK + EXT
M = 144

VMEM = pl.BlockSpec(memory_space=pltpu.VMEM)


def here():
    return lax.axis_index("z"), lax.axis_index("c")


def load_kernel(a, g, a_out, g_out, sems):
    copies = [pltpu.make_async_copy(x, y, sems.at[i]) for i, (x, y) in enumerate(((a, a_out), (g, g_out)))]
    for copy in copies:
        copy.start()
    for copy in copies:
        copy.wait()


def prep_kernel(a_own, a_oth, g_own, g_oth, out1, out2, mine, sums):
    z, c = here()
    a0 = a_own[...]
    a1 = a_oth[...]
    even = jnp.where(c == 0, a0, a1)
    odd = jnp.where(c == 0, a1, a0)
    g = jnp.concatenate([g_own[...], g_oth[...]], axis=0)
    i = lax.broadcasted_iota(jnp.int32, (CH, CH), 0)
    m = lax.broadcasted_iota(jnp.int32, (CH, CH), 1)
    source = 32 * ((m % 32) // 4) + 4 * (m // 32) + m % 4
    by_chip = jnp.where(i == source, 1.0, 0.0).astype(BF16)
    ordered = jnp.dot(g, by_chip, preferred_element_type=F32).astype(BF16)
    sums[...] = lax.dot_general(ordered, g, (((0,), (0,)), ((), ())), preferred_element_type=F32)

    def piece(chip):
        return sums[pl.ds(pl.multiple_of((chip % 8) * 32, 32), 32), :]

    step = 1 - 2 * c
    for d, out in ((1, out1), (2, out2)):
        out[:ROW, :] = even
        out[ROW : 2 * ROW, :] = odd
        out[2 * ROW : 2 * ROW + 32, :] = piece(z + 8 + d * step).astype(BF16)
        out[2 * ROW + 32 :, :] = piece(z + 8 + (d + 2) * step).astype(BF16)
    mine[...] = piece(z)


def shifts(x):
    pos = lax.broadcasted_iota(jnp.int32, (ROW, CH), 0) % 64
    xf = x.astype(F32)
    return (
        jnp.where(pos == 0, 0.0, pltpu.roll(xf, 1, 0)).astype(BF16),
        x,
        jnp.where(pos == 63, 0.0, pltpu.roll(xf, ROW - 1, 0)).astype(BF16),
    )


def selection(t):
    z, c = here()
    m = lax.broadcasted_iota(jnp.int32, (M, CH), 0)
    lane = lax.broadcasted_iota(jnp.int32, (M, CH), 1)
    owner = jnp.where(m < 128, m // 8, m - 128)
    within = jnp.where(m < 128, m % 8, 8)
    channel = owner * M + within + (z * 2 + c) * 9 - lane
    return jnp.where(channel == t * CH, 1.0, 0.0).astype(BF16)


def nt(a, b):
    return lax.dot_general(a, b, (((1,), (1,)), ((), ())), preferred_element_type=F32)


def main_kernel(a_own, a_oth, r1, s1, r2, s2, r3, s3, r4, s4, mine, out, v, sel, lt, ext, gs):
    z, c = here()
    chip = (lax.axis_index("y") * 2 + lax.axis_index("xh")) * 8 + z
    step = 1 - 2 * c

    def put(x, row):
        at = pl.ds(pl.multiple_of(row * ROW, ROW), ROW)
        for kx, moved in enumerate(shifts(x)):
            v[kx, at, :] = moved

    put(a_own[...], 8 + c)
    put(a_oth[...], 9 - c)
    for d, r, s in ((1, r1, s1), (2, r2, s2), (3, r3, s3), (4, r4, s4)):
        for half in range(2):
            put(r[half * ROW : half * ROW + ROW, :], 8 - 2 * d * step + half)
            put(s[half * ROW : half * ROW + ROW, :], 8 + 2 * d * step + half)
    for t in range(9):
        sel[t] = selection(t)
    top = (7 - 2 * chip + 128) % 128
    bottom = (6 - 2 * chip + 128) % 128
    lane = lax.broadcasted_iota(jnp.int32, (M, 256), 1)
    for n in range(8):
        sums = []
        for ky in range(3):
            acc = None
            for kx in range(3):
                part = nt(sel[3 * ky + kx], v[kx, ky * ROW + n * 256 : ky * ROW + n * 256 + 256, :])
                acc = part if acc is None else acc + part
            sums.append(acc)
        row = 2 * n + lane // ROW
        at_top = row == top
        at_bottom = row == bottom
        left = jnp.where(at_top, 0.0, sums[0]) + sums[1] + jnp.where(at_bottom, 0.0, sums[2])
        lanes = slice(n * 256, n * 256 + 256)
        lt[0, :, lanes] = jnp.where(at_top, 0.0, left).astype(BF16)
        lt[1, :, lanes] = left.astype(BF16)
        lt[2, :, lanes] = jnp.where(at_bottom, 0.0, left).astype(BF16)
    ext[...] = jnp.zeros_like(ext)
    for t in range(9):
        ky, kx = divmod(t, 3)
        res = jnp.dot(lt[ky], v[kx, ky * ROW : ky * ROW + 16 * ROW, :], preferred_element_type=F32)
        out[:, :, t * CH : t * CH + CH] = res[:128].reshape(16, 8, CH).astype(BF16)
        for q in range(16):
            ext[q, t // 2 : t // 2 + 1, (t % 2) * CH : (t % 2) * CH + CH] = res[128 + q : 129 + q]
    near = slice(2 * ROW, 2 * ROW + 32)
    far = slice(2 * ROW + 32, 2 * ROW + 64)
    total = mine[...]
    for ref, rows in ((r1, near), (s1, near), (r2, near), (s2, near), (r3, far), (s3, far)):
        total += ref[rows, :].astype(F32)
    gs[...] = total + jnp.where(c == 0, r4[far, :].astype(F32), s4[far, :].astype(F32))
    for q in range(8):
        for r in range(2):
            row = gs[pl.ds(q * 4 + r + 2 * c, 1), :]
            high = row.astype(BF16).astype(F32)
            for group in (0, 8):
                ext[group + q, 5:6, r * CH : r * CH + CH] = high
                ext[group + q, 6:7, r * CH : r * CH + CH] = row - high
    out[:, :, KK:] = ext[...].astype(BF16)


def end_kernel(coef, got, old_in, old_g, out_in, out_g):
    total = got[0].astype(F32)
    for q in range(1, 16):
        total += got[q].astype(F32)
    out_in[0:8, :] = 0.5 * old_in[0:8, :].astype(F32) + coef * total[:, :KK]
    last = 0.5 * old_in[8:9, :].astype(F32)
    for i in range(9):
        at = KK + (i % 2) * CH
        out_in[8:9, i * CH : i * CH + CH] = (
            last[:, i * CH : i * CH + CH] + coef * total[i // 2 : i // 2 + 1, at : at + CH]
        )
    for r in range(2):
        at = KK + r * CH
        out_g[r : r + 1, :] = 0.5 * old_g[r : r + 1, :] + coef * (
            total[5:6, at : at + CH] + total[6:7, at : at + CH]
        )


def call(kernel, shapes, args, scratch=(), flops=0, mib=8):
    return pl.pallas_call(
        kernel,
        out_shape=[jax.ShapeDtypeStruct(s, d) for s, d in shapes],
        in_specs=[VMEM] * len(args),
        out_specs=[VMEM] * len(shapes),
        scratch_shapes=[pltpu.VMEM(s, d) for s, d in scratch],
        cost_estimate=pl.CostEstimate(flops=flops, bytes_accessed=flops // 1000, transcendentals=0),
        compiler_params=pltpu.CompilerParams(vmem_limit_bytes=mib * 2**20),
    )(*args)


def swap(x):
    return lax.ppermute(x, "c", [(0, 1), (1, 0)])


def along(x, d):
    pairs = []
    for chip in range(64):
        pairs.append((2 * chip, 2 * ((chip + d) % 64)))
        pairs.append((2 * chip + 1, 2 * ((chip - d) % 64) + 1))
    return lax.ppermute(x, SPACE, pairs)


def per_device(activations, out_grads, old_input_factor, old_grad_factor):
    images, rows_here, columns_here, _ = activations.shape
    positions = images * lax.axis_size("dp") * rows_here * lax.axis_size(SPACE) * columns_here
    a = activations.reshape(ROW, CH)
    g = out_grads.reshape(ROW, CH)
    a_oth = swap(a)
    g_oth = swap(g)
    a_own, g_own = pl.pallas_call(
        load_kernel,
        out_shape=[jax.ShapeDtypeStruct((ROW, CH), BF16)] * 2,
        in_specs=[pl.BlockSpec(memory_space=pltpu.HBM)] * 2,
        out_specs=[VMEM] * 2,
        scratch_shapes=[pltpu.SemaphoreType.DMA((2,))],
        compiler_params=pltpu.CompilerParams(vmem_limit_bytes=2**20),
        name="load",
    )(a, g)
    sent1, sent2, mine = call(
        prep_kernel,
        [((320, CH), BF16)] * 2 + [((32, CH), F32)],
        (a_own, a_oth, g_own, g_oth),
        scratch=[((CH, CH), F32)],
        flops=1_000_000_000,
    )
    r1 = along(sent1, 1)
    r2 = along(sent2, 2)
    r3 = along(r1, 2)
    r4 = along(r2, 2)
    moved = []
    for r in (r1, r2, r3, r4):
        moved += [r, swap(r)]
    (parts,) = call(
        main_kernel,
        [((16, 8, WIDE), BF16)],
        (a_own, a_oth, *moved, mine),
        scratch=[
            ((3, 18 * ROW, CH), BF16),
            ((9, M, CH), BF16),
            ((3, M, 16 * ROW), BF16),
            ((16, 8, EXT), F32),
            ((32, CH), F32),
        ],
        flops=4_000_000_000,
        mib=24,
    )
    arrived = lax.all_to_all(parts, Q, 0, 0, tiled=True)
    return tuple(
        call(
            lambda *refs: end_kernel(0.5 / positions, *refs),
            [((9, KK), F32), ((2, CH), F32)],
            (arrived, old_input_factor, old_grad_factor),
        )
    )


def solution(mesh):
    finer = Mesh(
        mesh.devices.reshape(mesh.shape["dp"], 4, 2, 8, 2),
        ("dp", "y", "xh", "z", "c"),
    )

    return jax.shard_map(
        per_device,
        mesh=finer,
        in_specs=(
            P("dp", SPACE, None, None),
            P("dp", SPACE, None, None),
            P(DP_SPACE, None),
            P(SPACE, None),
        ),
        out_specs=(P(DP_SPACE, None), P(SPACE, None)),
        check_vma=False,
    )
```

time: 73.7 us -> 58.9 us (0.80)
  blocking collectives: 49 us -> 16.9 us
  waiting for transfers between devices: 3.32 us -> 14.8 us
  starting transfers between devices: 7.35 us -> 17.8 us
  Pallas kernels: 11.4 us -> 6.68 us
  local copies, waits for them, and re-layouts: 0.64 us -> 1.69 us
    all_to_all x1 -> x0, blocking collectives: 27.4 us -> none  [per_device(): got = lax.all_to_all(sent, 'z', 0, 0, tiled=True)]
    ppermute x3 -> x10, waiting for transfers between devices: 3.32 us -> 14.8 us  [the longest x4 13.4 us: along(): return lax.ppermute(x, SPACE, pairs)]
    ppermute x3 -> x10, starting transfers between devices: 7.35 us -> 17.8 us  [the longest x4 9.31 us: along(): return lax.ppermute(x, SPACE, pairs)]
    pallas_call x3 -> x4, Pallas kernels: 11.4 us -> 6.68 us  [the longest x3 6.53 us: call(): pl.pallas_call(kernel, out_shape=[jax.ShapeDtypeStruct(s, d) for s, d in...]
    all_to_all x1, blocking collectives: 21.5 us -> 16.9 us  [per_device(): arrived = lax.all_to_all(parts, Q, 0, 0, tiled=True)]
    unnamed x8, local copies, waits for them, and re-layouts: 0.64 us -> 1.69 us
  transfers between devices with their start and end apart: 3 -> 10, of which waited for: 2 -> 3; matrix products, arithmetic and copies ran while one was open for 1% -> 0% of each run, Pallas kernels for 0% -> 0%
where the time goes in v2:
time: 58.9 us; the launch traced here: 58.7 us
  starting transfers between devices  17.8 us (30%)
  blocking collectives  16.9 us (29%)
  waiting for transfers between devices  14.8 us (25%)
  Pallas kernels  6.68 us (11%)
  local copies, waits for them, and re-layouts  1.69 us (3%)
  between operations  0.72 us (1%)
    all_to_all x1, blocking collectives, per_device(): arrived = lax.all_to_all(parts, Q, 0, 0, tiled=True)  16.9 us
    ppermute x4, waiting for transfers between devices, along(): return lax.ppermute(x, SPACE, pairs)  13.4 us
    ppermute x4, starting transfers between devices, along(): return lax.ppermute(x, SPACE, pairs)  9.31 us
    ppermute x6, starting transfers between devices, swap(): return lax.ppermute(x, 'c', [(0, 1), (1, 0)])  8.53 us
    pallas_call x3, Pallas kernels, call(): pl.pallas_call(kernel, out_shape=[jax.ShapeDtypeStruct(s, d) for s, d in...  6.53 us
    unnamed x8, local copies, waits for them, and re-layouts  1.69 us
    ppermute x6, waiting for transfers between devices, swap(): return lax.ppermute(x, 'c', [(0, 1), (1, 0)])  1.39 us
  transfers between devices with their start and end apart: 10, of which 3 were waited for; matrix products, arithmetic and copies ran while one was open for 0% of the time, Pallas kernels for 0%

profile of v2, /device:TPU:32, one launch (start us, length us, event | category | flops | bytes accessed | tf_op | source)
XLA Modules:
  0.0 58.7 jit_solution(12090855484089455447)
XLA Ops:
  0.6 0.1 collective-permute-start
  0.7 0.5 collective-permute-start.1
  1.2 0.8 %copy-done.1 = bf16[2,1,64,256]{3,2,1,0:T(8,128)(2,1)S(1)} copy-done((bf16[2,1,64,256]{3,2,1,0:T(8,128)(2,1)S(1)}, bf16[2,1,64,256]{3,2,1,0:T(8,128)(2,1)}, u32[]{:S(2)}) %copy-start.1) | copy-done | bytes 65560
  2.1 0.8 %copy-done.2 = bf16[2,1,64,256]{3,2,1,0:T(8,128)(2,1)S(1)} copy-done((bf16[2,1,64,256]{3,2,1,0:T(8,128)(2,1)S(1)}, bf16[2,1,64,256]{3,2,1,0:T(8,128)(2,1)}, u32[]{:S(2)}) %copy-start.2) | copy-done | bytes 65560
  2.9 0.2 load.1
  3.1 0.0 collective-permute-done.a_oth
  3.1 0.5 shard_map.59
  3.6 2.0 %collective-permute-start.2 = (bf16[320,256]{1,0:T(8,128)(2,1)S(1)}, bf16[320,256]{1,0:T(8,128)(2,1)S(1)}, u32[]{:S(2)}, u32[]{:S(2)}) collective-permute-start(bf16[320,256]{1,0:T(8,128)(2,1)S(1)} %get-tuple-element.9), channel_id=1, source_target_pairs={{0,2},{1,127},{2,4},{3,1},{4,6},{5,3},{6,8},{7,5},{8,10},{9,7},{10... | collective-permute-start | bytes 491528 | tf_op jit(solution)/shard_map/ppermute | solution.py:186
  5.5 4.5 %collective-permute-start.4 = (bf16[320,256]{1,0:T(8,128)(2,1)S(1)}, bf16[320,256]{1,0:T(8,128)(2,1)S(1)}, u32[]{:S(2)}, u32[]{:S(2)}) collective-permute-start(bf16[320,256]{1,0:T(8,128)(2,1)S(1)} %get-tuple-element.10), channel_id=1, source_target_pairs={{0,4},{1,125},{2,6},{3,127},{4,8},{5,1},{6,10},{7,3},{8,12},{9,5},... | collective-permute-start | bytes 491528 | tf_op jit(solution)/shard_map/ppermute | solution.py:186
  10.0 0.0 collective-permute-done.2.r1
  10.0 2.8 %collective-permute-start.6 = (bf16[320,256]{1,0:T(8,128)(2,1)S(1)}, bf16[320,256]{1,0:T(8,128)(2,1)S(1)}, u32[]{:S(2)}, u32[]{:S(2)}) collective-permute-start(bf16[320,256]{1,0:T(8,128)(2,1)S(1)} %collective-permute-done.2.r1), channel_id=1, source_target_pairs={{0,4},{1,125},{2,6},{3,127},{4,8},{5,1},{6,10},{7,3},{8,12},{9,5},... | collective-permute-start | bytes 491528 | tf_op jit(solution)/shard_map/ppermute | solution.py:186
  12.9 6.8 %collective-permute-done.4.r2 = bf16[320,256]{1,0:T(8,128)(2,1)S(1)} collective-permute-done((bf16[320,256]{1,0:T(8,128)(2,1)S(1)}, bf16[320,256]{1,0:T(8,128)(2,1)S(1)}, u32[]{:S(2)}, u32[]{:S(2)}) %collective-permute-start.4) | collective-permute-done | bytes 163872 | tf_op jit(solution)/shard_map/ppermute | solution.py:186
  19.6 0.0 collective-permute-start.8
  19.6 7.4 %collective-permute-start.3 = (bf16[320,256]{1,0:T(8,128)(2,1)S(1)}, bf16[320,256]{1,0:T(8,128)(2,1)S(1)}, u32[]{:S(2)}, u32[]{:S(2)}) collective-permute-start(bf16[320,256]{1,0:T(8,128)(2,1)S(1)} %collective-permute-done.2.r1), channel_id=1, source_target_pairs={{0,1},{1,0},{2,3},{3,2},{4,5},{5,4},{6,7},{7,6},{8,9},{9,8},{10,11... | collective-permute-start | bytes 491528 | tf_op jit(solution)/shard_map/ppermute | solution.py:178
  27.1 0.0 collective-permute-done.6.r3
  27.1 0.5 collective-permute-start.7
  27.6 6.6 %collective-permute-done.8.r4 = bf16[320,256]{1,0:T(8,128)(2,1)S(1)} collective-permute-done((bf16[320,256]{1,0:T(8,128)(2,1)S(1)}, bf16[320,256]{1,0:T(8,128)(2,1)S(1)}, u32[]{:S(2)}, u32[]{:S(2)}) %collective-permute-start.8) | collective-permute-done | bytes 163872 | tf_op jit(solution)/shard_map/ppermute | solution.py:186
  34.2 0.0 collective-permute-done.3.s1
  34.2 1.4 %collective-permute-done.9.s4 = bf16[320,256]{1,0:T(8,128)(2,1)S(1)} collective-permute-done((bf16[320,256]{1,0:T(8,128)(2,1)S(1)}, bf16[320,256]{1,0:T(8,128)(2,1)S(1)}, u32[]{:S(2)}, u32[]{:S(2)}) %collective-permute-start.9) | collective-permute-done | bytes 163872 | tf_op jit(solution)/shard_map/ppermute | solution.py:178
  35.6 5.3 %shard_map.60 = bf16[16,8,2816]{2,1,0:T(8,128)(2,1)S(1)} custom-call(bf16[128,256]{1,0:T(8,128)(2,1)S(1)} %get-tuple-element.7.a_own, bf16[128,256]{1,0:T(8,128)(2,1)S(1)} %collective-permute-done.a_oth, bf16[320,256]{1,0:T(8,128)(2,1)S(1)} %collective-permute-done.2.r1, bf16[320,256]{1,0:T(8,128)(2,1)S(1)} %collective-permute-done.3.s1, ...), custom_call_target="tpu_custom_call" | custom-call | flops 4000000000 | bytes 4000000 | tf_op jit(solution)/shard_map/pallas_call | solution.py:166
  40.9 0.0 copy-start
  40.9 0.0 copy-start.3
  40.9 16.9 %all_to_all.5.refs_0_ = bf16[16,8,2816]{2,1,0:T(8,128)(2,1)S(1)} all-to-all(bf16[16,8,2816]{2,1,0:T(8,128)(2,1)S(1)} %shard_map.60), channel_id=1, replica_groups=mesh['dp'=2,'y'=4,'xh'=2,'z'=8,'c'=2] {'dp','y','xh'}, dimensions={0} | all-to-all | bytes 1441792 | tf_op jit(solution)/shard_map/all_to_all | solution.py:233
  57.9 0.8 %shard_map.61 = (f32[9,2304]{1,0:T(8,128)}, f32[2,256]{1,0:T(2,128)}) custom-call(bf16[16,8,2816]{2,1,0:T(8,128)(2,1)S(1)} %all_to_all.5.refs_0_, bf16[9,2304]{1,0:T(8,128)(2,1)S(1)} %copy-done, f32[2,256]{1,0:T(2,128)S(1)} %copy-done.3), custom_call_target="tpu_custom_call" | custom-call | tf_op jit(solution)/shard_map/pallas_call | solution.py:166
  (9 shorter events, 0.0 us)
Async XLA Ops:
  0.6 2.4 %collective-permute-start = (bf16[128,256]{1,0:T(8,128)(2,1)}, bf16[128,256]{1,0:T(8,128)(2,1)S(1)}, u32[]{:S(2)}, u32[]{:S(2)}) collective-permute-start(bf16[128,256]{1,0:T(8,128)(2,1)} %bitcast.2), channel_id=1, source_target_pairs={{0,1},{1,0},{2,3},{3,2},{4,5},{5,4},{6,7},{7,6},{8,9},{9,8},{10,11... | collective-permute-start | bytes 196616 | tf_op jit(solution)/shard_map/ppermute | solution.py:178
  0.7 2.4 %collective-permute-start.1 = (bf16[128,256]{1,0:T(8,128)(2,1)}, bf16[128,256]{1,0:T(8,128)(2,1)S(1)}, u32[]{:S(2)}, u32[]{:S(2)}) collective-permute-start(bf16[128,256]{1,0:T(8,128)(2,1)} %bitcast.4), channel_id=1, source_target_pairs={{0,1},{1,0},{2,3},{3,2},{4,5},{5,4},{6,7},{7,6},{8,9},{9,8},{10,11... | collective-permute-start | bytes 196616 | tf_op jit(solution)/shard_map/ppermute | solution.py:178
  1.2 0.8 %copy-start.1 = (bf16[2,1,64,256]{3,2,1,0:T(8,128)(2,1)S(1)}, bf16[2,1,64,256]{3,2,1,0:T(8,128)(2,1)}, u32[]{:S(2)}) copy-start(bf16[2,1,64,256]{3,2,1,0:T(8,128)(2,1)} %param.4) | copy-start | bytes 196612
  2.1 0.8 %copy-start.2 = (bf16[2,1,64,256]{3,2,1,0:T(8,128)(2,1)S(1)}, bf16[2,1,64,256]{3,2,1,0:T(8,128)(2,1)}, u32[]{:S(2)}) copy-start(bf16[2,1,64,256]{3,2,1,0:T(8,128)(2,1)} %param.5) | copy-start | bytes 196612
  3.6 6.5 %collective-permute-start.2 = (bf16[320,256]{1,0:T(8,128)(2,1)S(1)}, bf16[320,256]{1,0:T(8,128)(2,1)S(1)}, u32[]{:S(2)}, u32[]{:S(2)}) collective-permute-start(bf16[320,256]{1,0:T(8,128)(2,1)S(1)} %get-tuple-element.9), channel_id=1, source_target_pairs={{0,2},{1,127},{2,4},{3,1},{4,6},{5,3},{6,8},{7,5},{8,10},{9,7},{10... | collective-permute-start | bytes 491528 | tf_op jit(solution)/shard_map/ppermute | solution.py:186
  5.5 14.1 %collective-permute-start.4 = (bf16[320,256]{1,0:T(8,128)(2,1)S(1)}, bf16[320,256]{1,0:T(8,128)(2,1)S(1)}, u32[]{:S(2)}, u32[]{:S(2)}) collective-permute-start(bf16[320,256]{1,0:T(8,128)(2,1)S(1)} %get-tuple-element.10), channel_id=1, source_target_pairs={{0,4},{1,125},{2,6},{3,127},{4,8},{5,1},{6,10},{7,3},{8,12},{9,5},... | collective-permute-start | bytes 491528 | tf_op jit(solution)/shard_map/ppermute | solution.py:186
  10.0 17.0 %collective-permute-start.6 = (bf16[320,256]{1,0:T(8,128)(2,1)S(1)}, bf16[320,256]{1,0:T(8,128)(2,1)S(1)}, u32[]{:S(2)}, u32[]{:S(2)}) collective-permute-start(bf16[320,256]{1,0:T(8,128)(2,1)S(1)} %collective-permute-done.2.r1), channel_id=1, source_target_pairs={{0,4},{1,125},{2,6},{3,127},{4,8},{5,1},{6,10},{7,3},{8,12},{9,5},... | collective-permute-start | bytes 491528 | tf_op jit(solution)/shard_map/ppermute | solution.py:186
  19.6 14.6 %collective-permute-start.8 = (bf16[320,256]{1,0:T(8,128)(2,1)S(1)}, bf16[320,256]{1,0:T(8,128)(2,1)S(1)}, u32[]{:S(2)}, u32[]{:S(2)}) collective-permute-start(bf16[320,256]{1,0:T(8,128)(2,1)S(1)} %collective-permute-done.4.r2), channel_id=1, source_target_pairs={{0,4},{1,125},{2,6},{3,127},{4,8},{5,1},{6,10},{7,3},{8,12},{9,5},... | collective-permute-start | bytes 491528 | tf_op jit(solution)/shard_map/ppermute | solution.py:186
  19.6 14.6 %collective-permute-start.3 = (bf16[320,256]{1,0:T(8,128)(2,1)S(1)}, bf16[320,256]{1,0:T(8,128)(2,1)S(1)}, u32[]{:S(2)}, u32[]{:S(2)}) collective-permute-start(bf16[320,256]{1,0:T(8,128)(2,1)S(1)} %collective-permute-done.2.r1), channel_id=1, source_target_pairs={{0,1},{1,0},{2,3},{3,2},{4,5},{5,4},{6,7},{7,6},{8,9},{9,8},{10,11... | collective-permute-start | bytes 491528 | tf_op jit(solution)/shard_map/ppermute | solution.py:178
  27.1 7.2 %collective-permute-start.5 = (bf16[320,256]{1,0:T(8,128)(2,1)S(1)}, bf16[320,256]{1,0:T(8,128)(2,1)S(1)}, u32[]{:S(2)}, u32[]{:S(2)}) collective-permute-start(bf16[320,256]{1,0:T(8,128)(2,1)S(1)} %collective-permute-done.4.r2), channel_id=1, source_target_pairs={{0,1},{1,0},{2,3},{3,2},{4,5},{5,4},{6,7},{7,6},{8,9},{9,8},{10,11... | collective-permute-start | bytes 491528 | tf_op jit(solution)/shard_map/ppermute | solution.py:178
  27.1 7.2 %collective-permute-start.7 = (bf16[320,256]{1,0:T(8,128)(2,1)S(1)}, bf16[320,256]{1,0:T(8,128)(2,1)S(1)}, u32[]{:S(2)}, u32[]{:S(2)}) collective-permute-start(bf16[320,256]{1,0:T(8,128)(2,1)S(1)} %collective-permute-done.6.r3), channel_id=1, source_target_pairs={{0,1},{1,0},{2,3},{3,2},{4,5},{5,4},{6,7},{7,6},{8,9},{9,8},{10,11... | collective-permute-start | bytes 491528 | tf_op jit(solution)/shard_map/ppermute | solution.py:178
  34.2 1.4 %collective-permute-start.9 = (bf16[320,256]{1,0:T(8,128)(2,1)S(1)}, bf16[320,256]{1,0:T(8,128)(2,1)S(1)}, u32[]{:S(2)}, u32[]{:S(2)}) collective-permute-start(bf16[320,256]{1,0:T(8,128)(2,1)S(1)} %collective-permute-done.8.r4), channel_id=1, source_target_pairs={{0,1},{1,0},{2,3},{3,2},{4,5},{5,4},{6,7},{7,6},{8,9},{9,8},{10,11... | collective-permute-start | bytes 491528 | tf_op jit(solution)/shard_map/ppermute | solution.py:178
  40.9 17.0 %copy-start = (bf16[9,2304]{1,0:T(8,128)(2,1)S(1)}, bf16[9,2304]{1,0:T(8,128)(2,1)}, u32[]{:S(2)}) copy-start(bf16[9,2304]{1,0:T(8,128)(2,1)} %refs_1_.1) | copy-start | bytes 124420
  40.9 17.0 %copy-start.3 = (f32[2,256]{1,0:T(2,128)S(1)}, f32[2,256]{1,0:T(2,128)}, u32[]{:S(2)}) copy-start(f32[2,256]{1,0:T(2,128)} %refs_2_.1) | copy-start | bytes 6148

commit v3 on v2

v3 whole, which is shorter than its diff:
```python
import jax
import jax.numpy as jnp
from jax import lax
from jax.experimental import pallas as pl
from jax.experimental.pallas import tpu as pltpu
from jax.sharding import Mesh
from jax.sharding import PartitionSpec as P


SPACE = ("y", "xh", "z", "c")
DP_SPACE = ("dp", "y", "xh", "z", "c")
Q = ("dp", "y", "xh")
ROW = 128
CH = 256
KK = 9 * CH
F32 = jnp.float32
BF16 = jnp.bfloat16
EXT = 512
WIDE = KK + EXT
M = 144

VMEM = pl.BlockSpec(memory_space=pltpu.VMEM)


def here():
    return lax.axis_index("z"), lax.axis_index("c")


def prep_kernel(own, a_oth, g_oth, out1, out2, out3, pair, mine, sums):
    z, c = here()
    a0 = own[:ROW, :]
    a1 = a_oth[...]
    even = jnp.where(c == 0, a0, a1)
    odd = jnp.where(c == 0, a1, a0)
    g = jnp.concatenate([own[ROW:, :], g_oth[...]], axis=0)
    i = lax.broadcasted_iota(jnp.int32, (CH, CH), 0)
    m = lax.broadcasted_iota(jnp.int32, (CH, CH), 1)
    source = 32 * ((m % 32) // 4) + 4 * (m // 32) + m % 4
    by_chip = jnp.where(i == source, 1.0, 0.0).astype(BF16)
    ordered = jnp.dot(g, by_chip, preferred_element_type=F32).astype(BF16)
    sums[...] = lax.dot_general(ordered, g, (((0,), (0,)), ((), ())), preferred_element_type=F32)

    def piece(chip):
        return sums[pl.ds(pl.multiple_of((chip % 8) * 32, 32), 32), :]

    step = 1 - 2 * c
    for d, out in ((1, out1), (2, out2), (3, out3)):
        out[:ROW, :] = even
        out[ROW : 2 * ROW, :] = odd
        out[2 * ROW : 2 * ROW + 32, :] = piece(z + 8 + d * step).astype(BF16)
    out2[2 * ROW + 32 :, :] = piece(z + 8 + 4 * step).astype(BF16)
    pair[:ROW, :] = even
    pair[ROW:, :] = odd
    mine[...] = piece(z)


def shifts(x):
    pos = lax.broadcasted_iota(jnp.int32, (ROW, CH), 0) % 64
    xf = x.astype(F32)
    return (
        jnp.where(pos == 0, 0.0, pltpu.roll(xf, 1, 0)).astype(BF16),
        x,
        jnp.where(pos == 63, 0.0, pltpu.roll(xf, ROW - 1, 0)).astype(BF16),
    )


def selection(t):
    z, c = here()
    m = lax.broadcasted_iota(jnp.int32, (2 * M, CH), 0)
    lane = lax.broadcasted_iota(jnp.int32, (2 * M, CH), 1)
    core = jnp.where(m < M, c, 1 - c)
    m = jnp.where(m < M, m, m - M)
    owner = jnp.where(m < 128, m // 8, m - 128)
    within = jnp.where(m < 128, m % 8, 8)
    channel = owner * M + within + (z * 2 + core) * 9 - lane
    return jnp.where(channel == t * CH, 1.0, 0.0).astype(BF16)


def nt(a, b):
    return lax.dot_general(a, b, (((1,), (1,)), ((), ())), preferred_element_type=F32)


def fill(pairs, v):
    c = lax.axis_index("c")
    for i, pair in enumerate(pairs):
        at = jnp.where(c == 0, len(pairs) - 1 - i, i)
        for half in range(2):
            where = pl.ds(pl.multiple_of((2 * at + half) * ROW, ROW), ROW)
            for kx, moved in enumerate(shifts(pair[half * ROW : half * ROW + ROW, :])):
                v[kx, where, :] = moved


def left_side(near, pairs, v, sel, lt):
    z, c = here()
    chip = (lax.axis_index("y") * 2 + lax.axis_index("xh")) * 8 + z
    patches = 2 * pairs - 2
    start = 2 * chip + 1 + jnp.where(c == 0, -2 * (near + pairs - 1), 2 * near)
    top = (256 - start) % 128
    bottom = (255 - start) % 128
    lane = lax.broadcasted_iota(jnp.int32, (2 * M, 256), 1)
    for n in range(patches // 2):
        sums = []
        for ky in range(3):
            acc = None
            for kx in range(3):
                part = nt(sel[3 * ky + kx], v[kx, ky * ROW + n * 256 : ky * ROW + n * 256 + 256, :])
                acc = part if acc is None else acc + part
            sums.append(acc)
        row = 2 * n + lane // ROW
        at_top = row == top
        at_bottom = row == bottom
        left = jnp.where(at_top, 0.0, sums[0]) + sums[1] + jnp.where(at_bottom, 0.0, sums[2])
        lanes = slice(n * 256, n * 256 + 256)
        lt[0, :, lanes] = jnp.where(at_top, 0.0, left).astype(BF16)
        lt[1, :, lanes] = left.astype(BF16)
        lt[2, :, lanes] = jnp.where(at_bottom, 0.0, left).astype(BF16)


def product(t, patches, v, lt):
    ky, kx = divmod(t, 3)
    return jnp.dot(lt[ky], v[kx, ky * ROW : (ky + patches) * ROW, :], preferred_element_type=F32)


def near_kernel(pair, r1, r2, acc, sel, v, lt):
    fill((pair, r1, r2), v)
    for t in range(9):
        sel[t] = selection(t)
    left_side(0, 3, v, sel, lt)
    for t in range(9):
        acc[:, t * CH : t * CH + CH] = product(t, 4, v, lt)


def middle_kernel(r2, r3, sel, old, acc, v, lt):
    fill((r2, r3), v)
    left_side(2, 2, v, sel, lt)
    for t in range(9):
        lanes = slice(t * CH, t * CH + CH)
        acc[:, lanes] = old[:, lanes] + product(t, 2, v, lt)


def far_kernel(r1, r2, r3, r4, mine, sel, old, keep, give, v, lt, ext, gs):
    c = lax.axis_index("c")
    fill((r3, r4), v)
    left_side(3, 2, v, sel, lt)
    ext[...] = jnp.zeros_like(ext)
    for t in range(9):
        lanes = slice(t * CH, t * CH + CH)
        res = old[:, lanes] + product(t, 2, v, lt)
        keep[:, :, lanes] = res[:128].reshape(16, 8, CH)
        give[:, :, lanes] = res[M : M + 128].reshape(16, 8, CH).astype(BF16)
        lanes = slice((t % 2) * CH, (t % 2) * CH + CH)
        for side in range(2):
            for q in range(16):
                at = side * M + 128 + q
                ext[side, q, t // 2 : t // 2 + 1, lanes] = res[at : at + 1]
    total = jnp.where(c == 0, mine[...], 0.0)
    for ref in (r1, r2, r3):
        total += ref[2 * ROW : 2 * ROW + 32, :].astype(F32)
    gs[...] = total + jnp.where(c == 0, r4[2 * ROW + 32 :, :].astype(F32), 0.0)
    for side in range(2):
        core = c if side == 0 else 1 - c
        for q in range(8):
            for r in range(2):
                row = gs[pl.ds(q * 4 + r + 2 * core, 1), :]
                high = row.astype(BF16).astype(F32)
                for group in (0, 8):
                    ext[side, group + q, 5:6, r * CH : r * CH + CH] = high
                    ext[side, group + q, 6:7, r * CH : r * CH + CH] = row - high
    keep[:, :, KK:] = ext[0]
    give[:, :, KK:] = ext[1].astype(BF16)


def join_kernel(keep, got, out):
    for q in range(16):
        total = keep[q] + got[q].astype(F32)
        out[q, :, :] = total.astype(BF16)
        grad = total[5:6, KK:] + total[6:7, KK:]
        high = grad.astype(BF16).astype(F32)
        row = lax.broadcasted_iota(jnp.int32, (8, EXT), 0)
        tail = jnp.where(row == 5, high, jnp.where(row == 6, grad - high, total[:, KK:]))
        out[q, :, KK:] = tail.astype(BF16)


def end_kernel(coef, got, old_in, old_g, out_in, out_g):
    total = got[0].astype(F32)
    for q in range(1, 16):
        total += got[q].astype(F32)
    out_in[0:8, :] = 0.5 * old_in[0:8, :].astype(F32) + coef * total[:, :KK]
    last = 0.5 * old_in[8:9, :].astype(F32)
    for i in range(9):
        at = KK + (i % 2) * CH
        out_in[8:9, i * CH : i * CH + CH] = (
            last[:, i * CH : i * CH + CH] + coef * total[i // 2 : i // 2 + 1, at : at + CH]
        )
    for r in range(2):
        at = KK + r * CH
        out_g[r : r + 1, :] = 0.5 * old_g[r : r + 1, :] + coef * (
            total[5:6, at : at + CH] + total[6:7, at : at + CH]
        )


def call(kernel, shapes, args, scratch=(), flops=0, mib=8):
    return pl.pallas_call(
        kernel,
        out_shape=[jax.ShapeDtypeStruct(s, d) for s, d in shapes],
        in_specs=[VMEM] * len(args),
        out_specs=[VMEM] * len(shapes),
        scratch_shapes=[pltpu.VMEM(s, d) for s, d in scratch],
        cost_estimate=pl.CostEstimate(flops=flops, bytes_accessed=flops // 1000, transcendentals=0),
        compiler_params=pltpu.CompilerParams(vmem_limit_bytes=mib * 2**20),
    )(*args)


def swap(x):
    return lax.ppermute(x, "c", [(0, 1), (1, 0)])


def along(x, d):
    pairs = []
    for chip in range(64):
        pairs.append((2 * chip, 2 * ((chip + d) % 64)))
        pairs.append((2 * chip + 1, 2 * ((chip - d) % 64) + 1))
    return lax.ppermute(x, SPACE, pairs)


def per_device(activations, out_grads, old_input_factor, old_grad_factor):
    images, rows_here, columns_here, _ = activations.shape
    positions = images * lax.axis_size("dp") * rows_here * lax.axis_size(SPACE) * columns_here
    a = activations.reshape(ROW, CH)
    g = out_grads.reshape(ROW, CH)
    a_oth = swap(a)
    g_oth = swap(g)
    own = jnp.concatenate([a, g], axis=0)
    *sent, pair, mine = call(
        prep_kernel,
        [((rows, CH), BF16) for rows in (288, 320, 288, 2 * ROW)] + [((32, CH), F32)],
        (own, a_oth, g_oth),
        scratch=[((CH, CH), F32)],
        flops=1_000_000_000,
    )
    moved = [along(x, d) for d, x in enumerate(sent, 1)]
    moved.append(along(moved[1], 2))
    r1, r2, r3, r4 = moved
    acc, sel = call(
        near_kernel,
        [((2 * M, KK), F32), ((9, 2 * M, CH), BF16)],
        (pair, r1, r2),
        scratch=[((3, 6 * ROW, CH), BF16), ((3, 2 * M, 4 * ROW), BF16)],
        flops=2_000_000_000,
        mib=16,
    )
    (acc,) = call(
        middle_kernel,
        [((2 * M, KK), F32)],
        (r2, r3, sel, acc),
        scratch=[((3, 4 * ROW, CH), BF16), ((3, 2 * M, 2 * ROW), BF16)],
        flops=1_000_000_000,
        mib=16,
    )
    keep, give = call(
        far_kernel,
        [((16, 8, WIDE), F32), ((16, 8, WIDE), BF16)],
        (r1, r2, r3, r4, mine, sel, acc),
        scratch=[
            ((3, 4 * ROW, CH), BF16),
            ((3, 2 * M, 2 * ROW), BF16),
            ((2, 16, 8, EXT), F32),
            ((32, CH), F32),
        ],
        flops=1_000_000_000,
        mib=18,
    )
    got = swap(give)
    (parts,) = call(join_kernel, [((16, 8, WIDE), BF16)], (keep, got))
    arrived = lax.all_to_all(parts, Q, 0, 0, tiled=True)
    return tuple(
        call(
            lambda *refs: end_kernel(0.5 / positions, *refs),
            [((9, KK), F32), ((2, CH), F32)],
            (arrived, old_input_factor, old_grad_factor),
        )
    )


def solution(mesh):
    finer = Mesh(
        mesh.devices.reshape(mesh.shape["dp"], 4, 2, 8, 2),
        ("dp", "y", "xh", "z", "c"),
    )

    return jax.shard_map(
        per_device,
        mesh=finer,
        in_specs=(
            P("dp", SPACE, None, None),
            P("dp", SPACE, None, None),
            P(DP_SPACE, None),
            P(SPACE, None),
        ),
        out_specs=(P(DP_SPACE, None), P(SPACE, None)),
        check_vma=False,
    )
```

time: 58.9 us -> 53.1 us (0.902)
  starting transfers between devices: 17.8 us -> 9.09 us
  waiting for transfers between devices: 14.8 us -> 19.4 us
  local copies, waits for them, and re-layouts: 1.69 us -> 0.01 us
  other arithmetic: 0 us -> 0.88 us
    ppermute x6 -> x3, starting transfers between devices: 8.53 us -> 0.68 us  [swap(): return lax.ppermute(x, 'c', [(0, 1), (1, 0)])]
    ppermute x4, waiting for transfers between devices: 13.4 us -> 17 us  [along(): return lax.ppermute(x, SPACE, pairs)]
    unnamed x8 -> x4, local copies, waits for them, and re-layouts: 1.69 us -> 0.01 us
    ppermute x6 -> x3, waiting for transfers between devices: 1.39 us -> 2.41 us  [swap(): return lax.ppermute(x, 'c', [(0, 1), (1, 0)])]
    ppermute x4, starting transfers between devices: 9.31 us -> 8.4 us  [along(): return lax.ppermute(x, SPACE, pairs)]
    concatenate x0 -> x1, other arithmetic: none -> 0.88 us  [per_device(): own = jnp.concatenate([a, g], axis=0)]
    pallas_call x3 -> x6, Pallas kernels: 6.53 us -> 6.14 us  [call(): pl.pallas_call(kernel, out_shape=[jax.ShapeDtypeStruct(s, d) for s, d in...]
  transfers between devices with their start and end apart: 10 -> 7, of which waited for: 3 -> 6; matrix products, arithmetic and copies ran while one was open for 0% -> 2% of each run, Pallas kernels for 0% -> 6%
where the time goes in v3:
time: 53.1 us; the launch traced here: 53 us
  waiting for transfers between devices  19.4 us (37%)
  blocking collectives  16.8 us (32%)
  starting transfers between devices  9.09 us (17%)
  Pallas kernels  6.14 us (12%)
  other arithmetic  0.88 us (2%)
  between operations  0.7 us (1%)
    ppermute x4, waiting for transfers between devices, along(): return lax.ppermute(x, SPACE, pairs)  17 us
    all_to_all x1, blocking collectives, per_device(): arrived = lax.all_to_all(parts, Q, 0, 0, tiled=True)  16.8 us
    ppermute x4, starting transfers between devices, along(): return lax.ppermute(x, SPACE, pairs)  8.4 us
    pallas_call x6, Pallas kernels, call(): pl.pallas_call(kernel, out_shape=[jax.ShapeDtypeStruct(s, d) for s, d in...  6.14 us
    ppermute x3, waiting for transfers between devices, swap(): return lax.ppermute(x, 'c', [(0, 1), (1, 0)])  2.41 us
  transfers between devices with their start and end apart: 7, of which 6 were waited for; matrix products, arithmetic and copies ran while one was open for 2% of the time, Pallas kernels for 6%

profile of v3, /device:TPU:32, one launch (start us, length us, event | category | flops | bytes accessed | tf_op | source)
XLA Modules:
  0.0 53.0 jit_solution(17261432955733221422)
XLA Ops:
  0.6 0.1 collective-permute-start
  0.7 0.5 collective-permute-start.1
  1.2 0.9 %pad_maximum_fusion.own = bf16[256,256]{1,0:T(8,128)(2,1)S(1)} fusion(bf16[128,256]{1,0:T(8,128)(2,1)} %bitcast.5, bf16[128,256]{1,0:T(8,128)(2,1)} %bitcast.3), kind=kLoop, calls=%fused_computation | loop fusion | flops 262144 | bytes 262144 | tf_op jit(solution)/shard_map/concatenate | solution.py:233
  2.1 0.1 collective-permute-done.a_oth
  2.2 0.2 collective-permute-done.1.g_oth
  2.3 0.5 shard_map.59
  2.8 3.3 %collective-permute-start.3 = (bf16[320,256]{1,0:T(8,128)(2,1)S(1)}, bf16[320,256]{1,0:T(8,128)(2,1)S(1)}, u32[]{:S(2)}, u32[]{:S(2)}) collective-permute-start(bf16[320,256]{1,0:T(8,128)(2,1)S(1)} %get-tuple-element.12), channel_id=1, source_target_pairs={{0,4},{1,125},{2,6},{3,127},{4,8},{5,1},{6,10},{7,3},{8,12},{9,5},... | collective-permute-start | bytes 491528 | tf_op jit(solution)/shard_map/ppermute | solution.py:223
  6.2 3.1 %collective-permute-start.2 = (bf16[288,256]{1,0:T(8,128)(2,1)S(1)}, bf16[288,256]{1,0:T(8,128)(2,1)S(1)}, u32[]{:S(2)}, u32[]{:S(2)}) collective-permute-start(bf16[288,256]{1,0:T(8,128)(2,1)S(1)} %get-tuple-element.11), channel_id=1, source_target_pairs={{0,2},{1,127},{2,4},{3,1},{4,6},{5,3},{6,8},{7,5},{8,10},{9,7},{10... | collective-permute-start | bytes 442376 | tf_op jit(solution)/shard_map/ppermute | solution.py:223
  9.3 1.9 %collective-permute-start.4 = (bf16[288,256]{1,0:T(8,128)(2,1)S(1)}, bf16[288,256]{1,0:T(8,128)(2,1)S(1)}, u32[]{:S(2)}, u32[]{:S(2)}) collective-permute-start(bf16[288,256]{1,0:T(8,128)(2,1)S(1)} %get-tuple-element.13), channel_id=1, source_target_pairs={{0,6},{1,123},{2,8},{3,125},{4,10},{5,127},{6,12},{7,1},{8,14},{9,... | collective-permute-start | bytes 442376 | tf_op jit(solution)/shard_map/ppermute | solution.py:223
  11.2 7.0 %collective-permute-done.3.r2 = bf16[320,256]{1,0:T(8,128)(2,1)S(1)} collective-permute-done((bf16[320,256]{1,0:T(8,128)(2,1)S(1)}, bf16[320,256]{1,0:T(8,128)(2,1)S(1)}, u32[]{:S(2)}, u32[]{:S(2)}) %collective-permute-start.3) | collective-permute-done | bytes 163872 | tf_op jit(solution)/shard_map/ppermute | solution.py:223
  18.2 0.0 collective-permute-start.5
  18.3 0.0 collective-permute-done.2.r1
  18.3 2.0 %shard_map.60 = (f32[288,2304]{1,0:T(8,128)S(1)}, bf16[9,288,256]{2,1,0:T(8,128)(2,1)S(1)}) custom-call(bf16[256,256]{1,0:T(8,128)(2,1)S(1)} %get-tuple-element.15.pair, bf16[288,256]{1,0:T(8,128)(2,1)S(1)} %collective-permute-done.2.r1, bf16[320,256]{1,0:T(8,128)(2,1)S(1)} %collective-permute-done.3.r2), custom_call_target="tpu_custom_call" | custom-call | flops 2000000000 | bytes 2000000 | tf_op jit(solution)/shard_map/pallas_call | solution.py:203
  20.2 2.2 %collective-permute-done.4.r3 = bf16[288,256]{1,0:T(8,128)(2,1)S(1)} collective-permute-done((bf16[288,256]{1,0:T(8,128)(2,1)S(1)}, bf16[288,256]{1,0:T(8,128)(2,1)S(1)}, u32[]{:S(2)}, u32[]{:S(2)}) %collective-permute-start.4) | collective-permute-done | bytes 147488 | tf_op jit(solution)/shard_map/ppermute | solution.py:223
  22.4 1.3 %shard_map.61.old = f32[288,2304]{1,0:T(8,128)S(1)} custom-call(bf16[320,256]{1,0:T(8,128)(2,1)S(1)} %collective-permute-done.3.r2, bf16[288,256]{1,0:T(8,128)(2,1)S(1)} %collective-permute-done.4.r3, bf16[9,288,256]{2,1,0:T(8,128)(2,1)S(1)} %get-tuple-element.16.sel, f32[288,2304]{1,0:T(8,128)S(1)} %get-tuple-element.17.old), custom_call_target="tpu_custom_call" | custom-call | flops 1000000000 | bytes 1000000 | tf_op jit(solution)/shard_map/pallas_call | solution.py:203
  23.7 7.7 %collective-permute-done.5.r4 = bf16[320,256]{1,0:T(8,128)(2,1)S(1)} collective-permute-done((bf16[320,256]{1,0:T(8,128)(2,1)S(1)}, bf16[320,256]{1,0:T(8,128)(2,1)S(1)}, u32[]{:S(2)}, u32[]{:S(2)}) %collective-permute-start.5) | collective-permute-done | bytes 163872 | tf_op jit(solution)/shard_map/ppermute | solution.py:223
  31.4 1.4 %shard_map.62 = (f32[16,8,2816]{2,1,0:T(8,128)S(1)}, bf16[16,8,2816]{2,1,0:T(8,128)(2,1)S(1)}) custom-call(bf16[288,256]{1,0:T(8,128)(2,1)S(1)} %collective-permute-done.2.r1, bf16[320,256]{1,0:T(8,128)(2,1)S(1)} %collective-permute-done.3.r2, bf16[288,256]{1,0:T(8,128)(2,1)S(1)} %collective-permute-done.4.r3, ...), custom_call_target="tpu_custom_call" | custom-call | flops 1000000000 | bytes 1000000 | tf_op jit(solution)/shard_map/pallas_call | solution.py:203
  32.9 0.0 copy-start
  32.9 0.0 copy-start.1
  32.9 0.1 collective-permute-start.6
  33.0 2.2 %collective-permute-done.6.got = bf16[16,8,2816]{2,1,0:T(8,128)(2,1)S(1)} collective-permute-done((bf16[16,8,2816]{2,1,0:T(8,128)(2,1)S(1)}, bf16[16,8,2816]{2,1,0:T(8,128)(2,1)S(1)}, u32[]{:S(2)}, u32[]{:S(2)}) %collective-permute-start.6) | collective-permute-done | bytes 720928 | tf_op jit(solution)/shard_map/ppermute | solution.py:215
  35.2 0.2 shard_map.63
  35.4 16.8 %all_to_all.5.refs_0_ = bf16[16,8,2816]{2,1,0:T(8,128)(2,1)S(1)} all-to-all(bf16[16,8,2816]{2,1,0:T(8,128)(2,1)S(1)} %shard_map.63), channel_id=1, replica_groups=mesh['dp'=2,'y'=4,'xh'=2,'z'=8,'c'=2] {'dp','y','xh'}, dimensions={0} | all-to-all | bytes 1441792 | tf_op jit(solution)/shard_map/all_to_all | solution.py:275
  52.2 0.8 %shard_map.64 = (f32[9,2304]{1,0:T(8,128)}, f32[2,256]{1,0:T(2,128)}) custom-call(bf16[16,8,2816]{2,1,0:T(8,128)(2,1)S(1)} %all_to_all.5.refs_0_, bf16[9,2304]{1,0:T(8,128)(2,1)S(1)} %copy-done, f32[2,256]{1,0:T(2,128)S(1)} %copy-done.1), custom_call_target="tpu_custom_call" | custom-call | tf_op jit(solution)/shard_map/pallas_call | solution.py:203
  (2 shorter events, 0.0 us)
Async XLA Ops:
  0.6 1.6 %collective-permute-start = (bf16[128,256]{1,0:T(8,128)(2,1)}, bf16[128,256]{1,0:T(8,128)(2,1)S(1)}, u32[]{:S(2)}, u32[]{:S(2)}) collective-permute-start(bf16[128,256]{1,0:T(8,128)(2,1)} %bitcast.2), channel_id=1, source_target_pairs={{0,1},{1,0},{2,3},{3,2},{4,5},{5,4},{6,7},{7,6},{8,9},{9,8},{10,11... | collective-permute-start | bytes 196616 | tf_op jit(solution)/shard_map/ppermute | solution.py:215
  0.7 1.6 %collective-permute-start.1 = (bf16[128,256]{1,0:T(8,128)(2,1)}, bf16[128,256]{1,0:T(8,128)(2,1)S(1)}, u32[]{:S(2)}, u32[]{:S(2)}) collective-permute-start(bf16[128,256]{1,0:T(8,128)(2,1)} %bitcast.4), channel_id=1, source_target_pairs={{0,1},{1,0},{2,3},{3,2},{4,5},{5,4},{6,7},{7,6},{8,9},{9,8},{10,11... | collective-permute-start | bytes 196616 | tf_op jit(solution)/shard_map/ppermute | solution.py:215
  2.8 15.4 %collective-permute-start.3 = (bf16[320,256]{1,0:T(8,128)(2,1)S(1)}, bf16[320,256]{1,0:T(8,128)(2,1)S(1)}, u32[]{:S(2)}, u32[]{:S(2)}) collective-permute-start(bf16[320,256]{1,0:T(8,128)(2,1)S(1)} %get-tuple-element.12), channel_id=1, source_target_pairs={{0,4},{1,125},{2,6},{3,127},{4,8},{5,1},{6,10},{7,3},{8,12},{9,5},... | collective-permute-start | bytes 491528 | tf_op jit(solution)/shard_map/ppermute | solution.py:223
  6.2 12.1 %collective-permute-start.2 = (bf16[288,256]{1,0:T(8,128)(2,1)S(1)}, bf16[288,256]{1,0:T(8,128)(2,1)S(1)}, u32[]{:S(2)}, u32[]{:S(2)}) collective-permute-start(bf16[288,256]{1,0:T(8,128)(2,1)S(1)} %get-tuple-element.11), channel_id=1, source_target_pairs={{0,2},{1,127},{2,4},{3,1},{4,6},{5,3},{6,8},{7,5},{8,10},{9,7},{10... | collective-permute-start | bytes 442376 | tf_op jit(solution)/shard_map/ppermute | solution.py:223
  9.3 13.1 %collective-permute-start.4 = (bf16[288,256]{1,0:T(8,128)(2,1)S(1)}, bf16[288,256]{1,0:T(8,128)(2,1)S(1)}, u32[]{:S(2)}, u32[]{:S(2)}) collective-permute-start(bf16[288,256]{1,0:T(8,128)(2,1)S(1)} %get-tuple-element.13), channel_id=1, source_target_pairs={{0,6},{1,123},{2,8},{3,125},{4,10},{5,127},{6,12},{7,1},{8,14},{9,... | collective-permute-start | bytes 442376 | tf_op jit(solution)/shard_map/ppermute | solution.py:223
  18.2 13.2 %collective-permute-start.5 = (bf16[320,256]{1,0:T(8,128)(2,1)S(1)}, bf16[320,256]{1,0:T(8,128)(2,1)S(1)}, u32[]{:S(2)}, u32[]{:S(2)}) collective-permute-start(bf16[320,256]{1,0:T(8,128)(2,1)S(1)} %collective-permute-done.3.r2), channel_id=1, source_target_pairs={{0,4},{1,125},{2,6},{3,127},{4,8},{5,1},{6,10},{7,3},{8,12},{9,5},... | collective-permute-start | bytes 491528 | tf_op jit(solution)/shard_map/ppermute | solution.py:223
  32.9 19.3 %copy-start = (bf16[9,2304]{1,0:T(8,128)(2,1)S(1)}, bf16[9,2304]{1,0:T(8,128)(2,1)}, u32[]{:S(2)}) copy-start(bf16[9,2304]{1,0:T(8,128)(2,1)} %refs_1_.1) | copy-start | bytes 124420
  32.9 19.3 %copy-start.1 = (f32[2,256]{1,0:T(2,128)S(1)}, f32[2,256]{1,0:T(2,128)}, u32[]{:S(2)}) copy-start(f32[2,256]{1,0:T(2,128)} %refs_2_.1) | copy-start | bytes 6148
  32.9 2.3 %collective-permute-start.6 = (bf16[16,8,2816]{2,1,0:T(8,128)(2,1)S(1)}, bf16[16,8,2816]{2,1,0:T(8,128)(2,1)S(1)}, u32[]{:S(2)}, u32[]{:S(2)}) collective-permute-start(bf16[16,8,2816]{2,1,0:T(8,128)(2,1)S(1)} %get-tuple-element.19), channel_id=1, source_target_pairs={{0,1},{1,0},{2,3},{3,2},{4,5},{5,4},{6,7},{7,6},{8,9},{9,8},{10,11... | collective-permute-start | bytes 2162696 | tf_op jit(solution)/shard_map/ppermute | solution.py:215

commit v4 on v3

--- a/solution.py
+++ b/solution.py
@@ -90,20 +90,23 @@
                 v[kx, where, :] = moved
 
 
-def left_side(near, pairs, v, sel, lt):
+def left_side(near, pairs, v, sel, lt, first=0, count=2 * M):
     z, c = here()
     chip = (lax.axis_index("y") * 2 + lax.axis_index("xh")) * 8 + z
     patches = 2 * pairs - 2
     start = 2 * chip + 1 + jnp.where(c == 0, -2 * (near + pairs - 1), 2 * near)
     top = (256 - start) % 128
     bottom = (255 - start) % 128
-    lane = lax.broadcasted_iota(jnp.int32, (2 * M, 256), 1)
+    lane = lax.broadcasted_iota(jnp.int32, (count, 256), 1)
     for n in range(patches // 2):
         sums = []
         for ky in range(3):
             acc = None
             for kx in range(3):
-                part = nt(sel[3 * ky + kx], v[kx, ky * ROW + n * 256 : ky * ROW + n * 256 + 256, :])
+                part = nt(
+                    sel[3 * ky + kx, first : first + count, :],
+                    v[kx, ky * ROW + n * 256 : ky * ROW + n * 256 + 256, :],
+                )
                 acc = part if acc is None else acc + part
             sums.append(acc)
         row = 2 * n + lane // ROW
@@ -138,36 +141,39 @@
         acc[:, lanes] = old[:, lanes] + product(t, 2, v, lt)
 
 
-def far_kernel(r1, r2, r3, r4, mine, sel, old, keep, give, v, lt, ext, gs):
+def far_give_kernel(r1, r2, r3, r4, mine, sel, old, give, v, gs, lt, ext):
     c = lax.axis_index("c")
     fill((r3, r4), v)
-    left_side(3, 2, v, sel, lt)
-    ext[...] = jnp.zeros_like(ext)
-    for t in range(9):
-        lanes = slice(t * CH, t * CH + CH)
-        res = old[:, lanes] + product(t, 2, v, lt)
-        keep[:, :, lanes] = res[:128].reshape(16, 8, CH)
-        give[:, :, lanes] = res[M : M + 128].reshape(16, 8, CH).astype(BF16)
-        lanes = slice((t % 2) * CH, (t % 2) * CH + CH)
-        for side in range(2):
-            for q in range(16):
-                at = side * M + 128 + q
-                ext[side, q, t // 2 : t // 2 + 1, lanes] = res[at : at + 1]
+    left_side(3, 2, v, sel, lt, M, M)
     total = jnp.where(c == 0, mine[...], 0.0)
     for ref in (r1, r2, r3):
         total += ref[2 * ROW : 2 * ROW + 32, :].astype(F32)
     gs[...] = total + jnp.where(c == 0, r4[2 * ROW + 32 :, :].astype(F32), 0.0)
-    for side in range(2):
-        core = c if side == 0 else 1 - c
-        for q in range(8):
-            for r in range(2):
-                row = gs[pl.ds(q * 4 + r + 2 * core, 1), :]
-                high = row.astype(BF16).astype(F32)
-                for group in (0, 8):
-                    ext[side, group + q, 5:6, r * CH : r * CH + CH] = high
-                    ext[side, group + q, 6:7, r * CH : r * CH + CH] = row - high
-    keep[:, :, KK:] = ext[0]
-    give[:, :, KK:] = ext[1].astype(BF16)
+    finish(1 - c, M, old, v, lt, gs, give, ext)
+
+
+def far_keep_kernel(sel, old, v, gs, keep, lt, ext):
+    left_side(3, 2, v, sel, lt, 0, M)
+    finish(lax.axis_index("c"), 0, old, v, lt, gs, keep, ext)
+
+
+def finish(core, first, old, v, lt, gs, out, ext):
+    ext[...] = jnp.zeros_like(ext)
+    for t in range(9):
+        lanes = slice(t * CH, t * CH + CH)
+        res = old[first : first + M, lanes] + product(t, 2, v, lt)
+        out[:, :, lanes] = res[:128].reshape(16, 8, CH).astype(out.dtype)
+        lanes = slice((t % 2) * CH, (t % 2) * CH + CH)
+        for q in range(16):
+            ext[q, t // 2 : t // 2 + 1, lanes] = res[128 + q : 129 + q]
+    for q in range(8):
+        for r in range(2):
+            row = gs[pl.ds(q * 4 + r + 2 * core, 1), :]
+            high = row.astype(BF16).astype(F32)
+            for group in (0, 8):
+                ext[group + q, 5:6, r * CH : r * CH + CH] = high
+                ext[group + q, 6:7, r * CH : r * CH + CH] = row - high
+    out[:, :, KK:] = ext[...].astype(out.dtype)
 
 
 def join_kernel(keep, got, out):
@@ -257,20 +263,24 @@
         flops=1_000_000_000,
         mib=16,
     )
-    keep, give = call(
-        far_kernel,
-        [((16, 8, WIDE), F32), ((16, 8, WIDE), BF16)],
+    tail = [((3, M, 2 * ROW), BF16), ((16, 8, EXT), F32)]
+    give, v, gs = call(
+        far_give_kernel,
+        [((16, 8, WIDE), BF16), ((3, 4 * ROW, CH), BF16), ((32, CH), F32)],
         (r1, r2, r3, r4, mine, sel, acc),
-        scratch=[
-            ((3, 4 * ROW, CH), BF16),
-            ((3, 2 * M, 2 * ROW), BF16),
-            ((2, 16, 8, EXT), F32),
-            ((32, CH), F32),
-        ],
+        scratch=tail,
         flops=1_000_000_000,
-        mib=18,
+        mib=14,
     )
     got = swap(give)
+    (keep,) = call(
+        far_keep_kernel,
+        [((16, 8, WIDE), F32)],
+        (sel, acc, v, gs),
+        scratch=tail,
+        flops=1_000_000_000,
+        mib=14,
+    )
     (parts,) = call(join_kernel, [((16, 8, WIDE), BF16)], (keep, got))
     arrived = lax.all_to_all(parts, Q, 0, 0, tiled=True)
     return tuple(

time: 53.1 us -> 52.8 us (level)
  waiting for transfers between devices: 19.4 us -> 18.3 us
  Pallas kernels: 6.14 us -> 6.85 us
    ppermute x3, waiting for transfers between devices: 2.41 us -> 1.35 us  [swap(): return lax.ppermute(x, 'c', [(0, 1), (1, 0)])]
    pallas_call x6 -> x7, Pallas kernels: 6.14 us -> 6.85 us  [call(): pl.pallas_call(kernel, out_shape=[jax.ShapeDtypeStruct(s, d) for s, d in...]
  transfers between devices with their start and end apart: 7 -> 7, of which waited for: 6 -> 6; matrix products, arithmetic and copies ran while one was open for 2% -> 2% of each run, Pallas kernels for 6% -> 8%
where the time goes in v4:
time: 52.8 us; the launch traced here: 52.6 us
  waiting for transfers between devices  18.3 us (35%)
  blocking collectives  16.8 us (32%)
  starting transfers between devices  9.09 us (17%)
  Pallas kernels  6.85 us (13%)
  other arithmetic  0.88 us (2%)
  between operations  0.71 us (1%)
    ppermute x4, waiting for transfers between devices, along(): return lax.ppermute(x, SPACE, pairs)  17 us
    all_to_all x1, blocking collectives, per_device(): arrived = lax.all_to_all(parts, Q, 0, 0, tiled=True)  16.8 us
    ppermute x4, starting transfers between devices, along(): return lax.ppermute(x, SPACE, pairs)  8.4 us
    pallas_call x7, Pallas kernels, call(): pl.pallas_call(kernel, out_shape=[jax.ShapeDtypeStruct(s, d) for s, d in...  6.85 us
    ppermute x3, waiting for transfers between devices, swap(): return lax.ppermute(x, 'c', [(0, 1), (1, 0)])  1.35 us
  transfers between devices with their start and end apart: 7, of which 6 were waited for; matrix products, arithmetic and copies ran while one was open for 2% of the time, Pallas kernels for 8%

profile of v4, /device:TPU:32, one launch (start us, length us, event | category | flops | bytes accessed | tf_op | source)
XLA Modules:
  0.0 52.6 jit_solution(2921109163706702590)
XLA Ops:
  0.6 0.1 collective-permute-start
  0.7 0.5 collective-permute-start.1
  1.2 0.9 %pad_maximum_fusion.own = bf16[256,256]{1,0:T(8,128)(2,1)S(1)} fusion(bf16[128,256]{1,0:T(8,128)(2,1)} %bitcast.5, bf16[128,256]{1,0:T(8,128)(2,1)} %bitcast.3), kind=kLoop, calls=%fused_computation | loop fusion | flops 262144 | bytes 262144 | tf_op jit(solution)/shard_map/concatenate | solution.py:239
  2.1 0.1 collective-permute-done.a_oth
  2.2 0.2 collective-permute-done.1.g_oth
  2.3 0.5 shard_map.59
  2.8 3.3 %collective-permute-start.3 = (bf16[320,256]{1,0:T(8,128)(2,1)S(1)}, bf16[320,256]{1,0:T(8,128)(2,1)S(1)}, u32[]{:S(2)}, u32[]{:S(2)}) collective-permute-start(bf16[320,256]{1,0:T(8,128)(2,1)S(1)} %get-tuple-element.14), channel_id=1, source_target_pairs={{0,4},{1,125},{2,6},{3,127},{4,8},{5,1},{6,10},{7,3},{8,12},{9,5},... | collective-permute-start | bytes 491528 | tf_op jit(solution)/shard_map/ppermute | solution.py:229
  6.2 3.1 %collective-permute-start.2 = (bf16[288,256]{1,0:T(8,128)(2,1)S(1)}, bf16[288,256]{1,0:T(8,128)(2,1)S(1)}, u32[]{:S(2)}, u32[]{:S(2)}) collective-permute-start(bf16[288,256]{1,0:T(8,128)(2,1)S(1)} %get-tuple-element.13), channel_id=1, source_target_pairs={{0,2},{1,127},{2,4},{3,1},{4,6},{5,3},{6,8},{7,5},{8,10},{9,7},{10... | collective-permute-start | bytes 442376 | tf_op jit(solution)/shard_map/ppermute | solution.py:229
  9.3 1.9 %collective-permute-start.4 = (bf16[288,256]{1,0:T(8,128)(2,1)S(1)}, bf16[288,256]{1,0:T(8,128)(2,1)S(1)}, u32[]{:S(2)}, u32[]{:S(2)}) collective-permute-start(bf16[288,256]{1,0:T(8,128)(2,1)S(1)} %get-tuple-element.16), channel_id=1, source_target_pairs={{0,6},{1,123},{2,8},{3,125},{4,10},{5,127},{6,12},{7,1},{8,14},{9,... | collective-permute-start | bytes 442376 | tf_op jit(solution)/shard_map/ppermute | solution.py:229
  11.2 7.0 %collective-permute-done.3.r2 = bf16[320,256]{1,0:T(8,128)(2,1)S(1)} collective-permute-done((bf16[320,256]{1,0:T(8,128)(2,1)S(1)}, bf16[320,256]{1,0:T(8,128)(2,1)S(1)}, u32[]{:S(2)}, u32[]{:S(2)}) %collective-permute-start.3) | collective-permute-done | bytes 163872 | tf_op jit(solution)/shard_map/ppermute | solution.py:229
  18.2 0.0 collective-permute-start.5
  18.3 2.0 %shard_map.60 = (f32[288,2304]{1,0:T(8,128)S(1)}, bf16[9,288,256]{2,1,0:T(8,128)(2,1)S(1)}) custom-call(bf16[256,256]{1,0:T(8,128)(2,1)S(1)} %get-tuple-element.12.pair, bf16[288,256]{1,0:T(8,128)(2,1)S(1)} %collective-permute-done.2.r1, bf16[320,256]{1,0:T(8,128)(2,1)S(1)} %collective-permute-done.3.r2), custom_call_target="tpu_custom_call" | custom-call | flops 2000000000 | bytes 2000000 | tf_op jit(solution)/shard_map/pallas_call | solution.py:209
  20.2 2.2 %collective-permute-done.4.r3 = bf16[288,256]{1,0:T(8,128)(2,1)S(1)} collective-permute-done((bf16[288,256]{1,0:T(8,128)(2,1)S(1)}, bf16[288,256]{1,0:T(8,128)(2,1)S(1)}, u32[]{:S(2)}, u32[]{:S(2)}) %collective-permute-start.4) | collective-permute-done | bytes 147488 | tf_op jit(solution)/shard_map/ppermute | solution.py:229
  22.4 1.3 %shard_map.61.old = f32[288,2304]{1,0:T(8,128)S(1)} custom-call(bf16[320,256]{1,0:T(8,128)(2,1)S(1)} %collective-permute-done.3.r2, bf16[288,256]{1,0:T(8,128)(2,1)S(1)} %collective-permute-done.4.r3, bf16[9,288,256]{2,1,0:T(8,128)(2,1)S(1)} %get-tuple-element.15.sel, f32[288,2304]{1,0:T(8,128)S(1)} %get-tuple-element.17.old), custom_call_target="tpu_custom_call" | custom-call | flops 1000000000 | bytes 1000000 | tf_op jit(solution)/shard_map/pallas_call | solution.py:209
  23.7 7.7 %collective-permute-done.5.r4 = bf16[320,256]{1,0:T(8,128)(2,1)S(1)} collective-permute-done((bf16[320,256]{1,0:T(8,128)(2,1)S(1)}, bf16[320,256]{1,0:T(8,128)(2,1)S(1)}, u32[]{:S(2)}, u32[]{:S(2)}) %collective-permute-start.5) | collective-permute-done | bytes 163872 | tf_op jit(solution)/shard_map/ppermute | solution.py:229
  31.4 1.1 %shard_map.62 = (bf16[16,8,2816]{2,1,0:T(8,128)(2,1)S(1)}, bf16[3,512,256]{2,1,0:T(8,128)(2,1)S(1)}, f32[32,256]{1,0:T(8,128)S(1)}) custom-call(bf16[288,256]{1,0:T(8,128)(2,1)S(1)} %collective-permute-done.2.r1, bf16[320,256]{1,0:T(8,128)(2,1)S(1)} %collective-permute-done.3.r2, bf16[288,256]{1,0:T(8,128)(2,1)S(1)} %collective-permute-done.4.r3, ...), custom_call_target="tpu_custom_call" | custom-call | flops 1000000000 | bytes 1000000 | tf_op jit(solution)/shard_map/pallas_call | solution.py:209
  32.6 0.1 collective-permute-start.6
  32.7 1.0 %shard_map.63.keep = f32[16,8,2816]{2,1,0:T(8,128)S(1)} custom-call(bf16[9,288,256]{2,1,0:T(8,128)(2,1)S(1)} %get-tuple-element.15.sel, f32[288,2304]{1,0:T(8,128)S(1)} %shard_map.61.old, bf16[3,512,256]{2,1,0:T(8,128)(2,1)S(1)} %get-tuple-element.19.v, f32[32,256]{1,0:T(8,128)S(1)} %get-tuple-element.20.gs), custom_call_target="tpu_custom_call" | custom-call | flops 1000000000 | bytes 1000000 | tf_op jit(solution)/shard_map/pallas_call | solution.py:209
  33.7 0.0 copy-start
  33.7 0.0 copy-start.1
  33.7 1.1 %collective-permute-done.6.got = bf16[16,8,2816]{2,1,0:T(8,128)(2,1)S(1)} collective-permute-done((bf16[16,8,2816]{2,1,0:T(8,128)(2,1)S(1)}, bf16[16,8,2816]{2,1,0:T(8,128)(2,1)S(1)}, u32[]{:S(2)}, u32[]{:S(2)}) %collective-permute-start.6) | collective-permute-done | bytes 720928 | tf_op jit(solution)/shard_map/ppermute | solution.py:221
  34.8 0.2 shard_map.64
  35.1 16.8 %all_to_all.5.refs_0_ = bf16[16,8,2816]{2,1,0:T(8,128)(2,1)S(1)} all-to-all(bf16[16,8,2816]{2,1,0:T(8,128)(2,1)S(1)} %shard_map.64), channel_id=1, replica_groups=mesh['dp'=2,'y'=4,'xh'=2,'z'=8,'c'=2] {'dp','y','xh'}, dimensions={0} | all-to-all | bytes 1441792 | tf_op jit(solution)/shard_map/all_to_all | solution.py:285
  51.8 0.8 %shard_map.65 = (f32[9,2304]{1,0:T(8,128)}, f32[2,256]{1,0:T(2,128)}) custom-call(bf16[16,8,2816]{2,1,0:T(8,128)(2,1)S(1)} %all_to_all.5.refs_0_, bf16[9,2304]{1,0:T(8,128)(2,1)S(1)} %copy-done, f32[2,256]{1,0:T(2,128)S(1)} %copy-done.1), custom_call_target="tpu_custom_call" | custom-call | tf_op jit(solution)/shard_map/pallas_call | solution.py:209
  (3 shorter events, 0.0 us)
Async XLA Ops:
  0.6 1.6 %collective-permute-start = (bf16[128,256]{1,0:T(8,128)(2,1)}, bf16[128,256]{1,0:T(8,128)(2,1)S(1)}, u32[]{:S(2)}, u32[]{:S(2)}) collective-permute-start(bf16[128,256]{1,0:T(8,128)(2,1)} %bitcast.2), channel_id=1, source_target_pairs={{0,1},{1,0},{2,3},{3,2},{4,5},{5,4},{6,7},{7,6},{8,9},{9,8},{10,11... | collective-permute-start | bytes 196616 | tf_op jit(solution)/shard_map/ppermute | solution.py:221
  0.7 1.6 %collective-permute-start.1 = (bf16[128,256]{1,0:T(8,128)(2,1)}, bf16[128,256]{1,0:T(8,128)(2,1)S(1)}, u32[]{:S(2)}, u32[]{:S(2)}) collective-permute-start(bf16[128,256]{1,0:T(8,128)(2,1)} %bitcast.4), channel_id=1, source_target_pairs={{0,1},{1,0},{2,3},{3,2},{4,5},{5,4},{6,7},{7,6},{8,9},{9,8},{10,11... | collective-permute-start | bytes 196616 | tf_op jit(solution)/shard_map/ppermute | solution.py:221
  2.8 15.4 %collective-permute-start.3 = (bf16[320,256]{1,0:T(8,128)(2,1)S(1)}, bf16[320,256]{1,0:T(8,128)(2,1)S(1)}, u32[]{:S(2)}, u32[]{:S(2)}) collective-permute-start(bf16[320,256]{1,0:T(8,128)(2,1)S(1)} %get-tuple-element.14), channel_id=1, source_target_pairs={{0,4},{1,125},{2,6},{3,127},{4,8},{5,1},{6,10},{7,3},{8,12},{9,5},... | collective-permute-start | bytes 491528 | tf_op jit(solution)/shard_map/ppermute | solution.py:229
  6.2 12.1 %collective-permute-start.2 = (bf16[288,256]{1,0:T(8,128)(2,1)S(1)}, bf16[288,256]{1,0:T(8,128)(2,1)S(1)}, u32[]{:S(2)}, u32[]{:S(2)}) collective-permute-start(bf16[288,256]{1,0:T(8,128)(2,1)S(1)} %get-tuple-element.13), channel_id=1, source_target_pairs={{0,2},{1,127},{2,4},{3,1},{4,6},{5,3},{6,8},{7,5},{8,10},{9,7},{10... | collective-permute-start | bytes 442376 | tf_op jit(solution)/shard_map/ppermute | solution.py:229
  9.3 13.1 %collective-permute-start.4 = (bf16[288,256]{1,0:T(8,128)(2,1)S(1)}, bf16[288,256]{1,0:T(8,128)(2,1)S(1)}, u32[]{:S(2)}, u32[]{:S(2)}) collective-permute-start(bf16[288,256]{1,0:T(8,128)(2,1)S(1)} %get-tuple-element.16), channel_id=1, source_target_pairs={{0,6},{1,123},{2,8},{3,125},{4,10},{5,127},{6,12},{7,1},{8,14},{9,... | collective-permute-start | bytes 442376 | tf_op jit(solution)/shard_map/ppermute | solution.py:229
  18.2 13.2 %collective-permute-start.5 = (bf16[320,256]{1,0:T(8,128)(2,1)S(1)}, bf16[320,256]{1,0:T(8,128)(2,1)S(1)}, u32[]{:S(2)}, u32[]{:S(2)}) collective-permute-start(bf16[320,256]{1,0:T(8,128)(2,1)S(1)} %collective-permute-done.3.r2), channel_id=1, source_target_pairs={{0,4},{1,125},{2,6},{3,127},{4,8},{5,1},{6,10},{7,3},{8,12},{9,5},... | collective-permute-start | bytes 491528 | tf_op jit(solution)/shard_map/ppermute | solution.py:229
  32.6 2.3 %collective-permute-start.6 = (bf16[16,8,2816]{2,1,0:T(8,128)(2,1)S(1)}, bf16[16,8,2816]{2,1,0:T(8,128)(2,1)S(1)}, u32[]{:S(2)}, u32[]{:S(2)}) collective-permute-start(bf16[16,8,2816]{2,1,0:T(8,128)(2,1)S(1)} %get-tuple-element.21), channel_id=1, source_target_pairs={{0,1},{1,0},{2,3},{3,2},{4,5},{5,4},{6,7},{7,6},{8,9},{9,8},{10,11... | collective-permute-start | bytes 2162696 | tf_op jit(solution)/shard_map/ppermute | solution.py:221
  33.7 18.1 %copy-start = (bf16[9,2304]{1,0:T(8,128)(2,1)S(1)}, bf16[9,2304]{1,0:T(8,128)(2,1)}, u32[]{:S(2)}) copy-start(bf16[9,2304]{1,0:T(8,128)(2,1)} %refs_1_.1) | copy-start | bytes 124420
  33.7 18.1 %copy-start.1 = (f32[2,256]{1,0:T(2,128)S(1)}, f32[2,256]{1,0:T(2,128)}, u32[]{:S(2)}) copy-start(f32[2,256]{1,0:T(2,128)} %refs_2_.1) | copy-start | bytes 6148

commit v5 on v4

--- a/solution.py
+++ b/solution.py
@@ -26,7 +26,22 @@
     return lax.axis_index("z"), lax.axis_index("c")
 
 
-def prep_kernel(own, a_oth, g_oth, out1, out2, out3, pair, mine, sums):
+def routes(i):
+    sends = {}
+    for z in range(8):
+        side = 1 if z < 4 else -1
+        for c in range(2):
+            step = side * (i + 4 * c)
+            sends.setdefault((z + step) % 8, []).append((z, c, step))
+    table = []
+    for source in range(8):
+        table.append([])
+        for z, c, step in sorted(sends[source]):
+            table[-1].append((z, c, step))
+    return table
+
+
+def prep_kernel(own, a_oth, g_oth, out1, out2, out3, out4, pair, mine, sums):
     z, c = here()
     a0 = own[:ROW, :]
     a1 = a_oth[...]
@@ -43,12 +58,17 @@
     def piece(chip):
         return sums[pl.ds(pl.multiple_of((chip % 8) * 32, 32), 32), :]
 
-    step = 1 - 2 * c
-    for d, out in ((1, out1), (2, out2), (3, out3)):
+    def target(i):
+        found = 0
+        for source, two in enumerate(routes(i)):
+            for core, (to, _, _) in enumerate(two):
+                found = jnp.where((z == source) & (c == core), to, found)
+        return found
+
+    for i, out in ((1, out1), (2, out2), (3, out3), (4, out4)):
         out[:ROW, :] = even
         out[ROW : 2 * ROW, :] = odd
-        out[2 * ROW : 2 * ROW + 32, :] = piece(z + 8 + d * step).astype(BF16)
-    out2[2 * ROW + 32 :, :] = piece(z + 8 + 4 * step).astype(BF16)
+        out[2 * ROW :, :] = piece(target(i)).astype(BF16)
     pair[:ROW, :] = even
     pair[ROW:, :] = odd
     mine[...] = piece(z)
@@ -81,9 +101,9 @@
 
 
 def fill(pairs, v):
-    c = lax.axis_index("c")
+    z, _ = here()
     for i, pair in enumerate(pairs):
-        at = jnp.where(c == 0, len(pairs) - 1 - i, i)
+        at = jnp.where(z < 4, i, len(pairs) - 1 - i)
         for half in range(2):
             where = pl.ds(pl.multiple_of((2 * at + half) * ROW, ROW), ROW)
             for kx, moved in enumerate(shifts(pair[half * ROW : half * ROW + ROW, :])):
@@ -94,7 +114,8 @@
     z, c = here()
     chip = (lax.axis_index("y") * 2 + lax.axis_index("xh")) * 8 + z
     patches = 2 * pairs - 2
-    start = 2 * chip + 1 + jnp.where(c == 0, -2 * (near + pairs - 1), 2 * near)
+    step = 4 * c + near
+    start = 2 * chip + 1 + 2 * jnp.where(z < 4, step, 1 - step - pairs)
     top = (256 - start) % 128
     bottom = (255 - start) % 128
     lane = lax.broadcasted_iota(jnp.int32, (count, 256), 1)
@@ -124,36 +145,32 @@
     return jnp.dot(lt[ky], v[kx, ky * ROW : (ky + patches) * ROW, :], preferred_element_type=F32)
 
 
-def near_kernel(pair, r1, r2, acc, sel, v, lt):
-    fill((pair, r1, r2), v)
+def edges_kernel(pair, mid, r1, r3, r4, acc, sel, v1, v2, lt1, lt2):
+    _, c = here()
+    first = jnp.where(c == 0, pair[...], mid[: 2 * ROW, :])
+    fill((first, r1), v1)
+    fill((r3, r4), v2)
     for t in range(9):
         sel[t] = selection(t)
-    left_side(0, 3, v, sel, lt)
+    left_side(0, 2, v1, sel, lt1)
+    left_side(3, 2, v2, sel, lt2)
     for t in range(9):
-        acc[:, t * CH : t * CH + CH] = product(t, 4, v, lt)
-
-
-def middle_kernel(r2, r3, sel, old, acc, v, lt):
-    fill((r2, r3), v)
-    left_side(2, 2, v, sel, lt)
-    for t in range(9):
-        lanes = slice(t * CH, t * CH + CH)
-        acc[:, lanes] = old[:, lanes] + product(t, 2, v, lt)
+        acc[:, t * CH : t * CH + CH] = product(t, 2, v1, lt1) + product(t, 2, v2, lt2)
 
 
 def far_give_kernel(r1, r2, r3, r4, mine, sel, old, give, v, gs, lt, ext):
     c = lax.axis_index("c")
-    fill((r3, r4), v)
-    left_side(3, 2, v, sel, lt, M, M)
+    fill((r1, r2, r3), v)
+    left_side(1, 3, v, sel, lt, M, M)
     total = jnp.where(c == 0, mine[...], 0.0)
     for ref in (r1, r2, r3):
         total += ref[2 * ROW : 2 * ROW + 32, :].astype(F32)
-    gs[...] = total + jnp.where(c == 0, r4[2 * ROW + 32 :, :].astype(F32), 0.0)
+    gs[...] = total + jnp.where(c == 0, r4[2 * ROW :, :].astype(F32), 0.0)
     finish(1 - c, M, old, v, lt, gs, give, ext)
 
 
 def far_keep_kernel(sel, old, v, gs, keep, lt, ext):
-    left_side(3, 2, v, sel, lt, 0, M)
+    left_side(1, 3, v, sel, lt, 0, M)
     finish(lax.axis_index("c"), 0, old, v, lt, gs, keep, ext)
 
 
@@ -161,7 +178,7 @@
     ext[...] = jnp.zeros_like(ext)
     for t in range(9):
         lanes = slice(t * CH, t * CH + CH)
-        res = old[first : first + M, lanes] + product(t, 2, v, lt)
+        res = old[first : first + M, lanes] + product(t, 4, v, lt)
         out[:, :, lanes] = res[:128].reshape(16, 8, CH).astype(out.dtype)
         lanes = slice((t % 2) * CH, (t % 2) * CH + CH)
         for q in range(16):
@@ -221,11 +238,13 @@
     return lax.ppermute(x, "c", [(0, 1), (1, 0)])
 
 
-def along(x, d):
+def along(x, i):
     pairs = []
-    for chip in range(64):
-        pairs.append((2 * chip, 2 * ((chip + d) % 64)))
-        pairs.append((2 * chip + 1, 2 * ((chip - d) % 64) + 1))
+    for two in routes(i):
+        for core, (z, c, step) in enumerate(two):
+            for q in range(8):
+                target = 8 * q + z
+                pairs.append((2 * ((target + step) % 64) + core, 2 * target + c))
     return lax.ppermute(x, SPACE, pairs)
 
 
@@ -239,34 +258,25 @@
     own = jnp.concatenate([a, g], axis=0)
     *sent, pair, mine = call(
         prep_kernel,
-        [((rows, CH), BF16) for rows in (288, 320, 288, 2 * ROW)] + [((32, CH), F32)],
+        [((rows, CH), BF16) for rows in (288, 288, 288, 288, 2 * ROW)] + [((32, CH), F32)],
         (own, a_oth, g_oth),
         scratch=[((CH, CH), F32)],
         flops=1_000_000_000,
     )
-    moved = [along(x, d) for d, x in enumerate(sent, 1)]
-    moved.append(along(moved[1], 2))
-    r1, r2, r3, r4 = moved
+    r1, r2, r3, r4 = (along(x, i) for i, x in enumerate(sent, 1))
+    mid = swap(r4)
     acc, sel = call(
-        near_kernel,
+        edges_kernel,
         [((2 * M, KK), F32), ((9, 2 * M, CH), BF16)],
-        (pair, r1, r2),
-        scratch=[((3, 6 * ROW, CH), BF16), ((3, 2 * M, 4 * ROW), BF16)],
+        (pair, mid, r1, r3, r4),
+        scratch=[((3, 4 * ROW, CH), BF16)] * 2 + [((3, 2 * M, 2 * ROW), BF16)] * 2,
         flops=2_000_000_000,
         mib=16,
     )
-    (acc,) = call(
-        middle_kernel,
-        [((2 * M, KK), F32)],
-        (r2, r3, sel, acc),
-        scratch=[((3, 4 * ROW, CH), BF16), ((3, 2 * M, 2 * ROW), BF16)],
-        flops=1_000_000_000,
-        mib=16,
-    )
-    tail = [((3, M, 2 * ROW), BF16), ((16, 8, EXT), F32)]
+    tail = [((3, M, 4 * ROW), BF16), ((16, 8, EXT), F32)]
     give, v, gs = call(
         far_give_kernel,
-        [((16, 8, WIDE), BF16), ((3, 4 * ROW, CH), BF16), ((32, CH), F32)],
+        [((16, 8, WIDE), BF16), ((3, 6 * ROW, CH), BF16), ((32, CH), F32)],
         (r1, r2, r3, r4, mine, sel, acc),
         scratch=tail,
         flops=1_000_000_000,

time: 52.8 us -> 51.4 us (0.973)
  the two profiles are of different devices: /device:TPU:32 before, /device:TPU:64 now
where the time goes in v5:
time: 51.4 us; the launch traced here: 51.2 us
  blocking collectives  21.2 us (41%)
  starting transfers between devices  16.5 us (32%)
  Pallas kernels  6.49 us (13%)
  waiting for transfers between devices  5.32 us (10%)
  other arithmetic  0.88 us (2%)
  between operations  0.71 us (1%)
    all_to_all x1, blocking collectives, per_device(): arrived = lax.all_to_all(parts, Q, 0, 0, tiled=True)  21.2 us
    ppermute x4, starting transfers between devices, along(): return lax.ppermute(x, SPACE, pairs)  13.3 us
    pallas_call x6, Pallas kernels, call(): pl.pallas_call(kernel, out_shape=[jax.ShapeDtypeStruct(s, d) for s, d in...  6.49 us
    ppermute x4, waiting for transfers between devices, along(): return lax.ppermute(x, SPACE, pairs)  4.66 us
    ppermute x4, starting transfers between devices, swap(): return lax.ppermute(x, 'c', [(0, 1), (1, 0)])  3.21 us
  transfers between devices with their start and end apart: 8, of which 5 were waited for; matrix products, arithmetic and copies ran while one was open for 2% of the time, Pallas kernels for 7%

profile of v5, /device:TPU:64, one launch (start us, length us, event | category | flops | bytes accessed | tf_op | source)
XLA Modules:
  0.0 51.2 jit_solution(4128133541649115772)
XLA Ops:
  0.6 0.1 collective-permute-start
  0.7 0.5 collective-permute-start.1
  1.2 0.9 %pad_maximum_fusion.own = bf16[256,256]{1,0:T(8,128)(2,1)S(1)} fusion(bf16[128,256]{1,0:T(8,128)(2,1)} %bitcast.5, bf16[128,256]{1,0:T(8,128)(2,1)} %bitcast.3), kind=kLoop, calls=%fused_computation | loop fusion | flops 262144 | bytes 262144 | tf_op jit(solution)/shard_map/concatenate | solution.py:258
  2.1 0.1 collective-permute-done.a_oth
  2.2 0.2 collective-permute-done.1.g_oth
  2.3 0.5 shard_map.59
  2.8 5.5 %collective-permute-start.2 = (bf16[288,256]{1,0:T(8,128)(2,1)S(1)}, bf16[288,256]{1,0:T(8,128)(2,1)S(1)}, u32[]{:S(2)}, u32[]{:S(2)}) collective-permute-start(bf16[288,256]{1,0:T(8,128)(2,1)S(1)} %get-tuple-element.14), channel_id=1, source_target_pairs={{16,1},{32,17},{48,33},{64,49},{80,65},{96,81},{112,97},{0,113},{1... | collective-permute-start | bytes 442376 | tf_op jit(solution)/shard_map/ppermute | solution.py:248
  8.3 0.1 collective-permute-start.4
  8.4 5.5 %collective-permute-start.5 = (bf16[288,256]{1,0:T(8,128)(2,1)S(1)}, bf16[288,256]{1,0:T(8,128)(2,1)S(1)}, u32[]{:S(2)}, u32[]{:S(2)}) collective-permute-start(bf16[288,256]{1,0:T(8,128)(2,1)S(1)} %get-tuple-element.16), channel_id=1, source_target_pairs={{16,3},{32,19},{48,35},{64,51},{80,67},{96,83},{112,99},{0,115},{1... | collective-permute-start | bytes 442376 | tf_op jit(solution)/shard_map/ppermute | solution.py:248
  13.9 0.3 collective-permute-done.2.r4
  14.2 0.0 collective-permute-start.3
  14.2 2.2 %collective-permute-start.6 = (bf16[288,256]{1,0:T(8,128)(2,1)S(1)}, bf16[288,256]{1,0:T(8,128)(2,1)S(1)}, u32[]{:S(2)}, u32[]{:S(2)}) collective-permute-start(bf16[288,256]{1,0:T(8,128)(2,1)S(1)} %get-tuple-element.19), channel_id=1, source_target_pairs={{16,5},{32,21},{48,37},{64,53},{80,69},{96,85},{112,101},{0,117},{... | collective-permute-start | bytes 442376 | tf_op jit(solution)/shard_map/ppermute | solution.py:248
  16.4 4.4 %collective-permute-done.5.r3 = bf16[288,256]{1,0:T(8,128)(2,1)S(1)} collective-permute-done((bf16[288,256]{1,0:T(8,128)(2,1)S(1)}, bf16[288,256]{1,0:T(8,128)(2,1)S(1)}, u32[]{:S(2)}, u32[]{:S(2)}) %collective-permute-start.5) | collective-permute-done | bytes 147488 | tf_op jit(solution)/shard_map/ppermute | solution.py:248
  20.8 2.1 %shard_map.60 = (f32[288,2304]{1,0:T(8,128)S(1)}, bf16[9,288,256]{2,1,0:T(8,128)(2,1)S(1)}) custom-call(bf16[256,256]{1,0:T(8,128)(2,1)S(1)} %get-tuple-element.13.pair, bf16[288,256]{1,0:T(8,128)(2,1)S(1)} %collective-permute-done.3.mid, bf16[288,256]{1,0:T(8,128)(2,1)S(1)} %collective-permute-done.4.r1, bf16[288,256]{1,0:T(8,128)(2,1)S(1)} %collective-permute-done.5.r3, ...), custom_call_target="tpu_custom_call" | custom-call | flops 2000000000 | bytes 2000000 | tf_op jit(solution)/shard_map/pallas_call | solution.py:226
  22.9 0.0 collective-permute-done.6.r2
  22.9 1.5 %shard_map.61 = (bf16[16,8,2816]{2,1,0:T(8,128)(2,1)S(1)}, bf16[3,768,256]{2,1,0:T(8,128)(2,1)S(1)}, f32[32,256]{1,0:T(8,128)S(1)}) custom-call(bf16[288,256]{1,0:T(8,128)(2,1)S(1)} %collective-permute-done.4.r1, bf16[288,256]{1,0:T(8,128)(2,1)S(1)} %collective-permute-done.6.r2, bf16[288,256]{1,0:T(8,128)(2,1)S(1)} %collective-permute-done.5.r3, ...), custom_call_target="tpu_custom_call" | custom-call | flops 1000000000 | bytes 1000000 | tf_op jit(solution)/shard_map/pallas_call | solution.py:226
  24.5 2.6 %collective-permute-start.7 = (bf16[16,8,2816]{2,1,0:T(8,128)(2,1)S(1)}, bf16[16,8,2816]{2,1,0:T(8,128)(2,1)S(1)}, u32[]{:S(2)}, u32[]{:S(2)}) collective-permute-start(bf16[16,8,2816]{2,1,0:T(8,128)(2,1)S(1)} %get-tuple-element.23), channel_id=1, source_target_pairs={{0,1},{1,0},{2,3},{3,2},{4,5},{5,4},{6,7},{7,6},{8,9},{9,8},{10,11... | collective-permute-start | bytes 2162696 | tf_op jit(solution)/shard_map/ppermute | solution.py:238
  27.1 1.4 %shard_map.62.keep = f32[16,8,2816]{2,1,0:T(8,128)S(1)} custom-call(bf16[9,288,256]{2,1,0:T(8,128)(2,1)S(1)} %get-tuple-element.17.sel, f32[288,2304]{1,0:T(8,128)S(1)} %get-tuple-element.18.old, bf16[3,768,256]{2,1,0:T(8,128)(2,1)S(1)} %get-tuple-element.21.v, f32[32,256]{1,0:T(8,128)S(1)} %get-tuple-element.22.gs), custom_call_target="tpu_custom_call" | custom-call | flops 1000000000 | bytes 1000000 | tf_op jit(solution)/shard_map/pallas_call | solution.py:226
  28.5 0.4 collective-permute-done.7.got
  28.9 0.2 shard_map.63
  29.1 0.0 copy-start
  29.1 0.0 copy-start.1
  29.1 21.2 %all_to_all.5.refs_0_ = bf16[16,8,2816]{2,1,0:T(8,128)(2,1)S(1)} all-to-all(bf16[16,8,2816]{2,1,0:T(8,128)(2,1)S(1)} %shard_map.63), channel_id=1, replica_groups=mesh['dp'=2,'y'=4,'xh'=2,'z'=8,'c'=2] {'dp','y','xh'}, dimensions={0} | all-to-all | bytes 1441792 | tf_op jit(solution)/shard_map/all_to_all | solution.py:295
  50.4 0.8 %shard_map.64 = (f32[9,2304]{1,0:T(8,128)}, f32[2,256]{1,0:T(2,128)}) custom-call(bf16[16,8,2816]{2,1,0:T(8,128)(2,1)S(1)} %all_to_all.5.refs_0_, bf16[9,2304]{1,0:T(8,128)(2,1)S(1)} %copy-done, f32[2,256]{1,0:T(2,128)S(1)} %copy-done.1), custom_call_target="tpu_custom_call" | custom-call | tf_op jit(solution)/shard_map/pallas_call | solution.py:226
  (4 shorter events, 0.0 us)
Async XLA Ops:
  0.6 1.6 %collective-permute-start = (bf16[128,256]{1,0:T(8,128)(2,1)}, bf16[128,256]{1,0:T(8,128)(2,1)S(1)}, u32[]{:S(2)}, u32[]{:S(2)}) collective-permute-start(bf16[128,256]{1,0:T(8,128)(2,1)} %bitcast.2), channel_id=1, source_target_pairs={{0,1},{1,0},{2,3},{3,2},{4,5},{5,4},{6,7},{7,6},{8,9},{9,8},{10,11... | collective-permute-start | bytes 196616 | tf_op jit(solution)/shard_map/ppermute | solution.py:238
  0.7 1.6 %collective-permute-start.1 = (bf16[128,256]{1,0:T(8,128)(2,1)}, bf16[128,256]{1,0:T(8,128)(2,1)S(1)}, u32[]{:S(2)}, u32[]{:S(2)}) collective-permute-start(bf16[128,256]{1,0:T(8,128)(2,1)} %bitcast.4), channel_id=1, source_target_pairs={{0,1},{1,0},{2,3},{3,2},{4,5},{5,4},{6,7},{7,6},{8,9},{9,8},{10,11... | collective-permute-start | bytes 196616 | tf_op jit(solution)/shard_map/ppermute | solution.py:238
  2.8 11.4 %collective-permute-start.2 = (bf16[288,256]{1,0:T(8,128)(2,1)S(1)}, bf16[288,256]{1,0:T(8,128)(2,1)S(1)}, u32[]{:S(2)}, u32[]{:S(2)}) collective-permute-start(bf16[288,256]{1,0:T(8,128)(2,1)S(1)} %get-tuple-element.14), channel_id=1, source_target_pairs={{16,1},{32,17},{48,33},{64,49},{80,65},{96,81},{112,97},{0,113},{1... | collective-permute-start | bytes 442376 | tf_op jit(solution)/shard_map/ppermute | solution.py:248
  8.3 8.1 %collective-permute-start.4 = (bf16[288,256]{1,0:T(8,128)(2,1)S(1)}, bf16[288,256]{1,0:T(8,128)(2,1)S(1)}, u32[]{:S(2)}, u32[]{:S(2)}) collective-permute-start(bf16[288,256]{1,0:T(8,128)(2,1)S(1)} %get-tuple-element.15), channel_id=1, source_target_pairs={{16,7},{32,23},{48,39},{64,55},{80,71},{96,87},{112,103},{0,119},{... | collective-permute-start | bytes 442376 | tf_op jit(solution)/shard_map/ppermute | solution.py:248
  8.4 12.3 %collective-permute-start.5 = (bf16[288,256]{1,0:T(8,128)(2,1)S(1)}, bf16[288,256]{1,0:T(8,128)(2,1)S(1)}, u32[]{:S(2)}, u32[]{:S(2)}) collective-permute-start(bf16[288,256]{1,0:T(8,128)(2,1)S(1)} %get-tuple-element.16), channel_id=1, source_target_pairs={{16,3},{32,19},{48,35},{64,51},{80,67},{96,83},{112,99},{0,115},{1... | collective-permute-start | bytes 442376 | tf_op jit(solution)/shard_map/ppermute | solution.py:248
  14.2 6.6 %collective-permute-start.3 = (bf16[288,256]{1,0:T(8,128)(2,1)S(1)}, bf16[288,256]{1,0:T(8,128)(2,1)S(1)}, u32[]{:S(2)}, u32[]{:S(2)}) collective-permute-start(bf16[288,256]{1,0:T(8,128)(2,1)S(1)} %collective-permute-done.2.r4), channel_id=1, source_target_pairs={{0,1},{1,0},{2,3},{3,2},{4,5},{5,4},{6,7},{7,6},{8,9},{9,8},{10,11... | collective-permute-start | bytes 442376 | tf_op jit(solution)/shard_map/ppermute | solution.py:238
  14.2 8.7 %collective-permute-start.6 = (bf16[288,256]{1,0:T(8,128)(2,1)S(1)}, bf16[288,256]{1,0:T(8,128)(2,1)S(1)}, u32[]{:S(2)}, u32[]{:S(2)}) collective-permute-start(bf16[288,256]{1,0:T(8,128)(2,1)S(1)} %get-tuple-element.19), channel_id=1, source_target_pairs={{16,5},{32,21},{48,37},{64,53},{80,69},{96,85},{112,101},{0,117},{... | collective-permute-start | bytes 442376 | tf_op jit(solution)/shard_map/ppermute | solution.py:248
  24.5 4.4 %collective-permute-start.7 = (bf16[16,8,2816]{2,1,0:T(8,128)(2,1)S(1)}, bf16[16,8,2816]{2,1,0:T(8,128)(2,1)S(1)}, u32[]{:S(2)}, u32[]{:S(2)}) collective-permute-start(bf16[16,8,2816]{2,1,0:T(8,128)(2,1)S(1)} %get-tuple-element.23), channel_id=1, source_target_pairs={{0,1},{1,0},{2,3},{3,2},{4,5},{5,4},{6,7},{7,6},{8,9},{9,8},{10,11... | collective-permute-start | bytes 2162696 | tf_op jit(solution)/shard_map/ppermute | solution.py:238
  29.1 21.3 %copy-start = (bf16[9,2304]{1,0:T(8,128)(2,1)S(1)}, bf16[9,2304]{1,0:T(8,128)(2,1)}, u32[]{:S(2)}) copy-start(bf16[9,2304]{1,0:T(8,128)(2,1)} %refs_1_.1) | copy-start | bytes 124420
  29.1 21.3 %copy-start.1 = (f32[2,256]{1,0:T(2,128)S(1)}, f32[2,256]{1,0:T(2,128)}, u32[]{:S(2)}) copy-start(f32[2,256]{1,0:T(2,128)} %refs_2_.1) | copy-start | bytes 6148

commit v6 on v5

--- a/solution.py
+++ b/solution.py
@@ -145,13 +145,16 @@
     return jnp.dot(lt[ky], v[kx, ky * ROW : (ky + patches) * ROW, :], preferred_element_type=F32)
 
 
-def edges_kernel(pair, mid, r1, r3, r4, acc, sel, v1, v2, lt1, lt2):
+def sel_kernel(sel):
+    for t in range(9):
+        sel[t] = selection(t)
+
+
+def edges_kernel(pair, mid, r1, r3, r4, sel, acc, v1, v2, lt1, lt2):
     _, c = here()
     first = jnp.where(c == 0, pair[...], mid[: 2 * ROW, :])
     fill((first, r1), v1)
     fill((r3, r4), v2)
-    for t in range(9):
-        sel[t] = selection(t)
     left_side(0, 2, v1, sel, lt1)
     left_side(3, 2, v2, sel, lt2)
     for t in range(9):
@@ -265,10 +268,11 @@
     )
     r1, r2, r3, r4 = (along(x, i) for i, x in enumerate(sent, 1))
     mid = swap(r4)
-    acc, sel = call(
+    (sel,) = call(sel_kernel, [((9, 2 * M, CH), BF16)], ())
+    (acc,) = call(
         edges_kernel,
-        [((2 * M, KK), F32), ((9, 2 * M, CH), BF16)],
-        (pair, mid, r1, r3, r4),
+        [((2 * M, KK), F32)],
+        (pair, mid, r1, r3, r4, sel),
         scratch=[((3, 4 * ROW, CH), BF16)] * 2 + [((3, 2 * M, 2 * ROW), BF16)] * 2,
         flops=2_000_000_000,
         mib=16,

time: 51.4 us -> 51.6 us (level)
    pallas_call x6 -> x7, Pallas kernels: 6.49 us -> 6.63 us  [call(): pl.pallas_call(kernel, out_shape=[jax.ShapeDtypeStruct(s, d) for s, d in...]
where the time goes in v6:
time: 51.6 us; the launch traced here: 51.4 us
  blocking collectives  21.4 us (41%)
  starting transfers between devices  16.7 us (32%)
  Pallas kernels  6.63 us (13%)
  waiting for transfers between devices  5.05 us (10%)
  other arithmetic  0.88 us (2%)
  between operations  0.71 us (1%)
    all_to_all x1, blocking collectives, per_device(): arrived = lax.all_to_all(parts, Q, 0, 0, tiled=True)  21.4 us
    ppermute x4, starting transfers between devices, along(): return lax.ppermute(x, SPACE, pairs)  13.3 us
    pallas_call x7, Pallas kernels, call(): pl.pallas_call(kernel, out_shape=[jax.ShapeDtypeStruct(s, d) for s, d in...  6.63 us
    ppermute x4, waiting for transfers between devices, along(): return lax.ppermute(x, SPACE, pairs)  4.39 us
    ppermute x4, starting transfers between devices, swap(): return lax.ppermute(x, 'c', [(0, 1), (1, 0)])  3.44 us
  transfers between devices with their start and end apart: 8, of which 5 were waited for; matrix products, arithmetic and copies ran while one was open for 2% of the time, Pallas kernels for 7%

profile of v6, /device:TPU:64, one launch (start us, length us, event | category | flops | bytes accessed | tf_op | source)
XLA Modules:
  0.0 51.4 jit_solution(16621541053581661961)
XLA Ops:
  0.6 0.1 collective-permute-start
  0.7 0.5 collective-permute-start.1
  1.2 0.9 %pad_maximum_fusion.own = bf16[256,256]{1,0:T(8,128)(2,1)S(1)} fusion(bf16[128,256]{1,0:T(8,128)(2,1)} %bitcast.5, bf16[128,256]{1,0:T(8,128)(2,1)} %bitcast.3), kind=kLoop, calls=%fused_computation | loop fusion | flops 262144 | bytes 262144 | tf_op jit(solution)/shard_map/concatenate | solution.py:261
  2.1 0.1 collective-permute-done.a_oth
  2.2 0.2 collective-permute-done.1.g_oth
  2.3 0.5 shard_map.60
  2.8 5.5 %collective-permute-start.2 = (bf16[288,256]{1,0:T(8,128)(2,1)S(1)}, bf16[288,256]{1,0:T(8,128)(2,1)S(1)}, u32[]{:S(2)}, u32[]{:S(2)}) collective-permute-start(bf16[288,256]{1,0:T(8,128)(2,1)S(1)} %get-tuple-element.12), channel_id=1, source_target_pairs={{16,1},{32,17},{48,33},{64,49},{80,65},{96,81},{112,97},{0,113},{1... | collective-permute-start | bytes 442376 | tf_op jit(solution)/shard_map/ppermute | solution.py:251
  8.3 0.1 collective-permute-start.4
  8.4 5.5 %collective-permute-start.5 = (bf16[288,256]{1,0:T(8,128)(2,1)S(1)}, bf16[288,256]{1,0:T(8,128)(2,1)S(1)}, u32[]{:S(2)}, u32[]{:S(2)}) collective-permute-start(bf16[288,256]{1,0:T(8,128)(2,1)S(1)} %get-tuple-element.14), channel_id=1, source_target_pairs={{16,3},{32,19},{48,35},{64,51},{80,67},{96,83},{112,99},{0,115},{1... | collective-permute-start | bytes 442376 | tf_op jit(solution)/shard_map/ppermute | solution.py:251
  13.9 0.3 collective-permute-done.2.r4
  14.2 0.3 shard_map.59.sel
  14.5 2.2 %collective-permute-start.6 = (bf16[288,256]{1,0:T(8,128)(2,1)S(1)}, bf16[288,256]{1,0:T(8,128)(2,1)S(1)}, u32[]{:S(2)}, u32[]{:S(2)}) collective-permute-start(bf16[288,256]{1,0:T(8,128)(2,1)S(1)} %get-tuple-element.15), channel_id=1, source_target_pairs={{16,5},{32,21},{48,37},{64,53},{80,69},{96,85},{112,101},{0,117},{... | collective-permute-start | bytes 442376 | tf_op jit(solution)/shard_map/ppermute | solution.py:251
  16.7 4.1 %collective-permute-done.5.r3 = bf16[288,256]{1,0:T(8,128)(2,1)S(1)} collective-permute-done((bf16[288,256]{1,0:T(8,128)(2,1)S(1)}, bf16[288,256]{1,0:T(8,128)(2,1)S(1)}, u32[]{:S(2)}, u32[]{:S(2)}) %collective-permute-start.5) | collective-permute-done | bytes 147488 | tf_op jit(solution)/shard_map/ppermute | solution.py:251
  20.8 2.0 %shard_map.61.old = f32[288,2304]{1,0:T(8,128)S(1)} custom-call(bf16[256,256]{1,0:T(8,128)(2,1)S(1)} %get-tuple-element.11.pair, bf16[288,256]{1,0:T(8,128)(2,1)S(1)} %collective-permute-done.3.mid, bf16[288,256]{1,0:T(8,128)(2,1)S(1)} %collective-permute-done.4.r1, bf16[288,256]{1,0:T(8,128)(2,1)S(1)} %collective-permute-done.5.r3, ...), custom_call_target="tpu_custom_call" | custom-call | flops 2000000000 | bytes 2000000 | tf_op jit(solution)/shard_map/pallas_call | solution.py:229
  22.8 0.0 collective-permute-done.6.r2
  22.8 1.5 %shard_map.62 = (bf16[16,8,2816]{2,1,0:T(8,128)(2,1)S(1)}, bf16[3,768,256]{2,1,0:T(8,128)(2,1)S(1)}, f32[32,256]{1,0:T(8,128)S(1)}) custom-call(bf16[288,256]{1,0:T(8,128)(2,1)S(1)} %collective-permute-done.4.r1, bf16[288,256]{1,0:T(8,128)(2,1)S(1)} %collective-permute-done.6.r2, bf16[288,256]{1,0:T(8,128)(2,1)S(1)} %collective-permute-done.5.r3, ...), custom_call_target="tpu_custom_call" | custom-call | flops 1000000000 | bytes 1000000 | tf_op jit(solution)/shard_map/pallas_call | solution.py:229
  24.4 2.8 %collective-permute-start.7 = (bf16[16,8,2816]{2,1,0:T(8,128)(2,1)S(1)}, bf16[16,8,2816]{2,1,0:T(8,128)(2,1)S(1)}, u32[]{:S(2)}, u32[]{:S(2)}) collective-permute-start(bf16[16,8,2816]{2,1,0:T(8,128)(2,1)S(1)} %get-tuple-element.19), channel_id=1, source_target_pairs={{0,1},{1,0},{2,3},{3,2},{4,5},{5,4},{6,7},{7,6},{8,9},{9,8},{10,11... | collective-permute-start | bytes 2162696 | tf_op jit(solution)/shard_map/ppermute | solution.py:241
  27.2 1.4 %shard_map.63.keep = f32[16,8,2816]{2,1,0:T(8,128)S(1)} custom-call(bf16[9,288,256]{2,1,0:T(8,128)(2,1)S(1)} %shard_map.59.sel, f32[288,2304]{1,0:T(8,128)S(1)} %shard_map.61.old, bf16[3,768,256]{2,1,0:T(8,128)(2,1)S(1)} %get-tuple-element.17.v, f32[32,256]{1,0:T(8,128)S(1)} %get-tuple-element.18.gs), custom_call_target="tpu_custom_call" | custom-call | flops 1000000000 | bytes 1000000 | tf_op jit(solution)/shard_map/pallas_call | solution.py:229
  28.6 0.4 collective-permute-done.7.got
  29.0 0.2 shard_map.64
  29.2 0.0 copy-start
  29.2 0.0 copy-start.1
  29.2 21.4 %all_to_all.5.refs_0_ = bf16[16,8,2816]{2,1,0:T(8,128)(2,1)S(1)} all-to-all(bf16[16,8,2816]{2,1,0:T(8,128)(2,1)S(1)} %shard_map.64), channel_id=1, replica_groups=mesh['dp'=2,'y'=4,'xh'=2,'z'=8,'c'=2] {'dp','y','xh'}, dimensions={0} | all-to-all | bytes 1441792 | tf_op jit(solution)/shard_map/all_to_all | solution.py:299
  50.6 0.8 %shard_map.65 = (f32[9,2304]{1,0:T(8,128)}, f32[2,256]{1,0:T(2,128)}) custom-call(bf16[16,8,2816]{2,1,0:T(8,128)(2,1)S(1)} %all_to_all.5.refs_0_, bf16[9,2304]{1,0:T(8,128)(2,1)S(1)} %copy-done, f32[2,256]{1,0:T(2,128)S(1)} %copy-done.1), custom_call_target="tpu_custom_call" | custom-call | tf_op jit(solution)/shard_map/pallas_call | solution.py:229
  (5 shorter events, 0.0 us)
Async XLA Ops:
  0.6 1.6 %collective-permute-start = (bf16[128,256]{1,0:T(8,128)(2,1)}, bf16[128,256]{1,0:T(8,128)(2,1)S(1)}, u32[]{:S(2)}, u32[]{:S(2)}) collective-permute-start(bf16[128,256]{1,0:T(8,128)(2,1)} %bitcast.2), channel_id=1, source_target_pairs={{0,1},{1,0},{2,3},{3,2},{4,5},{5,4},{6,7},{7,6},{8,9},{9,8},{10,11... | collective-permute-start | bytes 196616 | tf_op jit(solution)/shard_map/ppermute | solution.py:241
  0.7 1.6 %collective-permute-start.1 = (bf16[128,256]{1,0:T(8,128)(2,1)}, bf16[128,256]{1,0:T(8,128)(2,1)S(1)}, u32[]{:S(2)}, u32[]{:S(2)}) collective-permute-start(bf16[128,256]{1,0:T(8,128)(2,1)} %bitcast.4), channel_id=1, source_target_pairs={{0,1},{1,0},{2,3},{3,2},{4,5},{5,4},{6,7},{7,6},{8,9},{9,8},{10,11... | collective-permute-start | bytes 196616 | tf_op jit(solution)/shard_map/ppermute | solution.py:241
  2.8 11.4 %collective-permute-start.2 = (bf16[288,256]{1,0:T(8,128)(2,1)S(1)}, bf16[288,256]{1,0:T(8,128)(2,1)S(1)}, u32[]{:S(2)}, u32[]{:S(2)}) collective-permute-start(bf16[288,256]{1,0:T(8,128)(2,1)S(1)} %get-tuple-element.12), channel_id=1, source_target_pairs={{16,1},{32,17},{48,33},{64,49},{80,65},{96,81},{112,97},{0,113},{1... | collective-permute-start | bytes 442376 | tf_op jit(solution)/shard_map/ppermute | solution.py:251
  8.3 8.3 %collective-permute-start.4 = (bf16[288,256]{1,0:T(8,128)(2,1)S(1)}, bf16[288,256]{1,0:T(8,128)(2,1)S(1)}, u32[]{:S(2)}, u32[]{:S(2)}) collective-permute-start(bf16[288,256]{1,0:T(8,128)(2,1)S(1)} %get-tuple-element.13), channel_id=1, source_target_pairs={{16,7},{32,23},{48,39},{64,55},{80,71},{96,87},{112,103},{0,119},{... | collective-permute-start | bytes 442376 | tf_op jit(solution)/shard_map/ppermute | solution.py:251
  8.4 12.3 %collective-permute-start.5 = (bf16[288,256]{1,0:T(8,128)(2,1)S(1)}, bf16[288,256]{1,0:T(8,128)(2,1)S(1)}, u32[]{:S(2)}, u32[]{:S(2)}) collective-permute-start(bf16[288,256]{1,0:T(8,128)(2,1)S(1)} %get-tuple-element.14), channel_id=1, source_target_pairs={{16,3},{32,19},{48,35},{64,51},{80,67},{96,83},{112,99},{0,115},{1... | collective-permute-start | bytes 442376 | tf_op jit(solution)/shard_map/ppermute | solution.py:251
  14.2 6.6 %collective-permute-start.3 = (bf16[288,256]{1,0:T(8,128)(2,1)S(1)}, bf16[288,256]{1,0:T(8,128)(2,1)S(1)}, u32[]{:S(2)}, u32[]{:S(2)}) collective-permute-start(bf16[288,256]{1,0:T(8,128)(2,1)S(1)} %collective-permute-done.2.r4), channel_id=1, source_target_pairs={{0,1},{1,0},{2,3},{3,2},{4,5},{5,4},{6,7},{7,6},{8,9},{9,8},{10,11... | collective-permute-start | bytes 442376 | tf_op jit(solution)/shard_map/ppermute | solution.py:241
  14.5 8.3 %collective-permute-start.6 = (bf16[288,256]{1,0:T(8,128)(2,1)S(1)}, bf16[288,256]{1,0:T(8,128)(2,1)S(1)}, u32[]{:S(2)}, u32[]{:S(2)}) collective-permute-start(bf16[288,256]{1,0:T(8,128)(2,1)S(1)} %get-tuple-element.15), channel_id=1, source_target_pairs={{16,5},{32,21},{48,37},{64,53},{80,69},{96,85},{112,101},{0,117},{... | collective-permute-start | bytes 442376 | tf_op jit(solution)/shard_map/ppermute | solution.py:251
  24.4 4.7 %collective-permute-start.7 = (bf16[16,8,2816]{2,1,0:T(8,128)(2,1)S(1)}, bf16[16,8,2816]{2,1,0:T(8,128)(2,1)S(1)}, u32[]{:S(2)}, u32[]{:S(2)}) collective-permute-start(bf16[16,8,2816]{2,1,0:T(8,128)(2,1)S(1)} %get-tuple-element.19), channel_id=1, source_target_pairs={{0,1},{1,0},{2,3},{3,2},{4,5},{5,4},{6,7},{7,6},{8,9},{9,8},{10,11... | collective-permute-start | bytes 2162696 | tf_op jit(solution)/shard_map/ppermute | solution.py:241
  29.2 21.4 %copy-start = (bf16[9,2304]{1,0:T(8,128)(2,1)S(1)}, bf16[9,2304]{1,0:T(8,128)(2,1)}, u32[]{:S(2)}) copy-start(bf16[9,2304]{1,0:T(8,128)(2,1)} %refs_1_.1) | copy-start | bytes 124420
  29.2 21.4 %copy-start.1 = (f32[2,256]{1,0:T(2,128)S(1)}, f32[2,256]{1,0:T(2,128)}, u32[]{:S(2)}) copy-start(f32[2,256]{1,0:T(2,128)} %refs_2_.1) | copy-start | bytes 6148
